TPU v7x, 32 devices: a whole 2x2x4 slice. The times are simulated.
32 devices in a mesh: seq: 16 (over z, x, core), head: 2 (over y).
Axes of the slice: x: 2, y: 2, z: 4, core: 2. Of those that a mesh axis runs over, the one named last changes fastest.
Arguments:
- x_proj: bfloat16 [4096, 8192], P(('seq', 'head')), may hold values from -6 to 6
- z_proj: bfloat16 [4096, 8192], P(('seq', 'head')), may hold values from -6 to 6
- b_proj: bfloat16 [4096, 1024], P(('seq', 'head')), may hold values from -6 to 6
- c_proj: bfloat16 [4096, 1024], P(('seq', 'head')), may hold values from -6 to 6
- dt_raw: bfloat16 [4096, 128], P(('seq', 'head')), may hold values from -3.2 to 3.2, as said below
- dt_bias: float32 [128], P('head'), may hold values from -6.3 to -1.2, as said below
- a_log: float32 [128], P('head'), as said below
- d_skip: float32 [128], P('head'), may hold values from 0.5 to 2
- conv_x: float32 [4, 8192], P(None, 'head'), may hold values from -3 to 3
- conv_bias_x: float32 [8192], P('head'), may hold values from -3 to 3
- conv_bc: float32 [4, 2, 1024], P(None, None, 'head'), may hold values from -3 to 3
- conv_bias_bc: float32 [2, 1024], P(None, 'head'), may hold values from -3 to 3
- norm_weight: float32 [8192], P('head'), may hold values from 0.25 to 1.75
- out_weight: bfloat16 [8192, 4096], P('head', 'seq'), may hold values from -0.0625 to 0.0625
Outputs:
- mixed: bfloat16 [4096, 4096], P(('seq', 'head'))
Inputs may be any that keep to these rules, and one draw needn't show every extreme that they name: `dt_raw`: A normal draw times 0.7 plus an offset common to each head and each aligned run of 256 tokens. `dt_bias`: the inverse softplus of a per-head step size between 0.002 and 0.25. Finite; exp(a_log) lies above 0.0 and at most 0.3.
All inputs are finite; a program needn't handle non-finite values.
Results may differ from a plain program's by a relative error of at most 0.014.
Values may be sent and summed in bfloat16 or wider, within the bound.
A program may use at most 192 MiB of HBM per device.

v0:
```python
import functools

import jax
import jax.numpy as jnp
from jax import lax
from jax.experimental import pallas as pl
from jax.experimental.pallas import tpu as pltpu
from jax.sharding import PartitionSpec as P

HEAD_DIM = 64
STATE = 128
GROUPS = 8
SPAN = 128
DI = 8192
HALO = 16
NT = (((1,), (1,)), ((), ()))


def entry_kernel(count, heads, *refs):
    x_in, z_in, b_in, c_in, dt_in = refs[:5]
    x_out, z_out, b_out, c_out, dt_out, x_halo, b_halo, c_halo = refs[5:13]
    send_sems, recv_sems, local_sems, halo_send, halo_recv = refs[13:]
    seq = lax.axis_index("seq")
    head = lax.axis_index("head")
    rows = x_in.shape[0]
    barrier = pltpu.get_barrier_semaphore()
    last_head = head == heads - 1
    gives_halo = jnp.logical_and(last_head, seq < count - 1)
    takes_halo = seq > 0
    for step in range(1, heads):
        peer = lax.rem(head + step, heads)
        pl.semaphore_signal(
            barrier, inc=1, device_id=(seq, peer), device_id_type=pl.DeviceIdType.MESH
        )

    @pl.when(takes_halo)
    def _():
        pl.semaphore_signal(
            barrier,
            inc=1,
            device_id=(seq - 1, heads - 1),
            device_id_type=pl.DeviceIdType.MESH,
        )

    pl.semaphore_wait(barrier, heads - 1 + jnp.where(gives_halo, heads, 0))

    def columns(ref, width, which):
        return ref.at[:, pl.ds(pl.multiple_of(which * width, 128), width)]

    mine = pl.ds(pl.multiple_of(head * rows, 16), rows)
    plan = (
        (b_in, b_out, True),
        (c_in, c_out, True),
        (dt_in, dt_out, False),
        (x_in, x_out, True),
        (z_in, z_out, True),
    )
    halos = ((x_in, x_halo), (b_in, b_halo), (c_in, c_halo))

    def halo_copy(index, peer):
        source, target = halos[index]
        width = target.shape[1]
        return pltpu.make_async_remote_copy(
            src_ref=source.at[pl.ds(rows - HALO, HALO), pl.ds(peer * width, width)],
            dst_ref=target,
            send_sem=halo_send.at[index, peer],
            recv_sem=halo_recv.at[index],
            device_id=(seq + 1, peer),
            device_id_type=pl.DeviceIdType.MESH,
        )

    @pl.when(gives_halo)
    def _():
        for index in range(len(halos)):
            for peer in range(heads):
                halo_copy(index, peer).start()

    copies = []
    for step in range(1, heads):
        peer = lax.rem(head + step, heads)
        for index, (source, target, split) in enumerate(plan):
            view = columns(source, target.shape[1], peer) if split else source
            copy = pltpu.make_async_remote_copy(
                src_ref=view,
                dst_ref=target.at[mine],
                send_sem=send_sems.at[index, step],
                recv_sem=recv_sems.at[index, step],
                device_id=(seq, peer),
                device_id_type=pl.DeviceIdType.MESH,
            )
            copy.start()
            copies.append(copy)
    for index, (source, target, split) in enumerate(plan):
        view = columns(source, target.shape[1], head) if split else source
        copy = pltpu.make_async_copy(view, target.at[mine], local_sems.at[index])
        copy.start()
        copies.append(copy)

    @pl.when(jnp.logical_not(takes_halo))
    def _():
        for _, target in halos:
            target[...] = jnp.zeros_like(target)

    @pl.when(takes_halo)
    def _():
        for index, (source, target) in enumerate(halos):
            pltpu.make_async_remote_copy(
                src_ref=source.at[pl.ds(rows - HALO, HALO), pl.ds(0, target.shape[1])],
                dst_ref=target,
                send_sem=halo_send.at[index, 0],
                recv_sem=halo_recv.at[index],
                device_id=(seq, head),
                device_id_type=pl.DeviceIdType.MESH,
            ).wait_recv()

    @pl.when(gives_halo)
    def _():
        for index in range(len(halos)):
            for peer in range(heads):
                halo_copy(index, peer).wait_send()

    for copy in copies:
        copy.wait()


def entry_exchange(x_proj, z_proj, b_proj, c_proj, dt_raw):
    count = lax.axis_size("seq")
    heads = lax.axis_size("head")
    rows = x_proj.shape[0] * heads
    x_cols = x_proj.shape[1] // heads
    bc_cols = b_proj.shape[1] // heads
    dtype = x_proj.dtype
    shapes = [
        (rows, x_cols),
        (rows, x_cols),
        (rows, bc_cols),
        (rows, bc_cols),
        (rows, dt_raw.shape[1]),
        (HALO, x_cols),
        (HALO, bc_cols),
        (HALO, bc_cols),
    ]
    return pl.pallas_call(
        functools.partial(entry_kernel, count, heads),
        out_shape=[jax.ShapeDtypeStruct(shape, dtype) for shape in shapes],
        in_specs=[pl.BlockSpec(memory_space=pl.ANY)] * 5,
        out_specs=[pl.BlockSpec(memory_space=pl.ANY)] * 5
        + [pl.BlockSpec(memory_space=pltpu.VMEM)] * 3,
        scratch_shapes=[
            pltpu.SemaphoreType.DMA((5, heads)),
            pltpu.SemaphoreType.DMA((5, heads)),
            pltpu.SemaphoreType.DMA((5,)),
            pltpu.SemaphoreType.DMA((3, heads)),
            pltpu.SemaphoreType.DMA((3,)),
        ],
        compiler_params=pltpu.CompilerParams(collective_id=0, has_side_effects=True),
        name="entry_exchange",
    )(x_proj, z_proj, b_proj, c_proj, dt_raw)


def conv_silu(value_ref, halo_ref, taps_ref, bias_ref, padded):
    tokens = value_ref.shape[0]
    taps = taps_ref.shape[0]
    padded[0:8, :] = halo_ref[HALO - 8 : HALO, :].astype(jnp.float32)
    padded[8 : 8 + tokens, :] = value_ref[...].astype(jnp.float32)
    total = bias_ref[...] + jnp.zeros(value_ref.shape, jnp.float32)
    for offset in range(taps):
        low = 8 - (taps - 1) + offset
        total = total + taps_ref[offset : offset + 1, :] * padded[low : low + tokens, :]
    return (total / (1.0 + jnp.exp(-total))).astype(jnp.bfloat16)


def local_kernel(
    x_ref,
    b_ref,
    c_ref,
    x_halo,
    b_halo,
    c_halo,
    x_taps,
    x_bias,
    b_taps,
    b_bias,
    c_taps,
    c_bias,
    step_t,
    cum_t,
    cum_c,
    skip_ref,
    y_ref,
    piece_ref,
    final_ref,
    c_out,
    x_pad,
    bc_pad,
    x_t,
    x_w,
    final,
):
    tokens, width = x_ref.shape
    heads = step_t.shape[0]
    blocks = tokens // SPAN
    x_conv = conv_silu(x_ref, x_halo, x_taps, x_bias, x_pad)
    b_conv = conv_silu(b_ref, b_halo, b_taps, b_bias, bc_pad)
    c_conv = conv_silu(c_ref, c_halo, c_taps, c_bias, bc_pad)
    c_out[...] = c_conv
    later = lax.broadcasted_iota(jnp.int32, (SPAN, SPAN), 0)
    earlier = lax.broadcasted_iota(jnp.int32, (SPAN, SPAN), 1)
    causal = later >= earlier
    for block in range(blocks):
        low = block * SPAN
        b_blk = b_conv[low : low + SPAN]
        c_blk = c_conv[low : low + SPAN]
        x_t[...] = x_conv[low : low + SPAN].astype(jnp.float32).T
        scores = lax.dot_general(c_blk, b_blk, NT, preferred_element_type=jnp.float32)
        for head in range(heads):
            rows = pl.ds(head * HEAD_DIM, HEAD_DIM)
            column = cum_c[0, low : low + SPAN, head : head + 1]
            row = cum_t[head : head + 1, low : low + SPAN]
            step = step_t[head : head + 1, low : low + SPAN]
            total = row[:, SPAN - 1 : SPAN]
            decays = jnp.exp(jnp.where(causal, column - row, -jnp.inf))
            mix = (decays * step * scores).astype(jnp.bfloat16)
            x_head = x_t[rows, :]
            product = lax.dot_general(
                x_head.astype(jnp.bfloat16), mix, NT, preferred_element_type=jnp.float32
            )
            y_ref[block, rows, :] = product + skip_ref[0, head : head + 1, :] * x_head
            x_w[rows, :] = (x_head * (step * jnp.exp(total - row))).astype(jnp.bfloat16)
        piece = jnp.dot(x_w[...], b_blk, preferred_element_type=jnp.float32)
        piece_ref[block] = piece
        if block == 0:
            final[...] = piece
        else:
            for head in range(heads):
                rows = pl.ds(head * HEAD_DIM, HEAD_DIM)
                decay = jnp.exp(cum_t[head : head + 1, low + SPAN - 1 : low + SPAN])
                final[rows, :] = decay * final[rows, :] + piece_ref[block, rows, :]
    final_ref[...] = final[...].astype(jnp.bfloat16)


def local_scan(x, b, c, halos, x_taps, x_bias, bc_taps, bc_bias, step_t, cum_t, cum_c, skip):
    tokens, x_cols = x.shape
    groups = b.shape[1] // STATE
    width = x_cols // groups
    heads = width // HEAD_DIM
    blocks = tokens // SPAN
    taps = x_taps.shape[0]

    def cols(rows, size):
        return pl.BlockSpec((rows, size), lambda g: (0, g))

    in_specs = [
        cols(tokens, width),
        cols(tokens, STATE),
        cols(tokens, STATE),
        cols(HALO, width),
        cols(HALO, STATE),
        cols(HALO, STATE),
        cols(taps, width),
        cols(1, width),
        cols(taps, STATE),
        cols(1, STATE),
        cols(taps, STATE),
        cols(1, STATE),
        pl.BlockSpec((heads, tokens), lambda g: (g, 0)),
        pl.BlockSpec((heads, tokens), lambda g: (g, 0)),
        pl.BlockSpec((1, tokens, heads), lambda g: (g, 0, 0)),
        pl.BlockSpec((1, heads, 1), lambda g: (g, 0, 0)),
    ]
    out_specs = [
        pl.BlockSpec((blocks, width, SPAN), lambda g: (0, g, 0)),
        pl.BlockSpec((blocks, width, STATE), lambda g: (0, g, 0)),
        pl.BlockSpec((width, STATE), lambda g: (g, 0)),
        cols(tokens, STATE),
    ]
    out_shape = [
        jax.ShapeDtypeStruct((blocks, x_cols, SPAN), jnp.float32),
        jax.ShapeDtypeStruct((blocks, x_cols, STATE), jnp.float32),
        jax.ShapeDtypeStruct((x_cols, STATE), jnp.bfloat16),
        jax.ShapeDtypeStruct((tokens, groups * STATE), jnp.bfloat16),
    ]
    return pl.pallas_call(
        local_kernel,
        grid=(groups,),
        in_specs=in_specs,
        out_specs=out_specs,
        out_shape=out_shape,
        scratch_shapes=[
            pltpu.VMEM((tokens + 8, width), jnp.float32),
            pltpu.VMEM((tokens + 8, STATE), jnp.float32),
            pltpu.VMEM((width, SPAN), jnp.float32),
            pltpu.VMEM((width, SPAN), jnp.bfloat16),
            pltpu.VMEM((width, STATE), jnp.float32),
        ],
        compiler_params=pltpu.CompilerParams(dimension_semantics=("arbitrary",)),
        cost_estimate=pl.CostEstimate(
            flops=20000000000, bytes_accessed=16000000, transcendentals=4000000
        ),
        name="local_scan",
    )(
        x,
        b,
        c,
        *halos,
        x_taps,
        x_bias[None],
        bc_taps[:, 0],
        bc_bias[0:1],
        bc_taps[:, 1],
        bc_bias[1:2],
        step_t,
        cum_t,
        cum_c,
        skip,
    )


def carry_kernel(start_ref, piece_ref, c_ref, cum_t, y_ref, z_ref, gain_ref, out_ref, running, y_t):
    tokens, width = z_ref.shape
    heads = cum_t.shape[0]
    blocks = tokens // SPAN
    running[...] = start_ref[...].astype(jnp.float32)
    for block in range(blocks):
        low = block * SPAN
        c_blk = c_ref[low : low + SPAN, :]
        carried = lax.dot_general(
            running[...].astype(jnp.bfloat16), c_blk, NT, preferred_element_type=jnp.float32
        )
        y_t[...] = carried
        for head in range(heads):
            rows = pl.ds(head * HEAD_DIM, HEAD_DIM)
            row = jnp.exp(cum_t[head : head + 1, low : low + SPAN])
            y_t[rows, :] = y_ref[block, rows, :] + y_t[rows, :] * row
            if block < blocks - 1:
                running[rows, :] = (
                    row[:, SPAN - 1 : SPAN] * running[rows, :] + piece_ref[block, rows, :]
                )
        gate = z_ref[low : low + SPAN, :].astype(jnp.float32)
        gated = y_t[...].T * (gate / (1.0 + jnp.exp(-gate)))
        mean = jnp.sum(gated * gated, axis=-1, keepdims=True) * (1.0 / width)
        normed = gated * lax.rsqrt(mean + 1.0)
        out_ref[low : low + SPAN, :] = (normed * gain_ref[...]).astype(jnp.bfloat16)


def carry_norm(start, pieces, c_conv, cum_t, y_t, z, gain):
    tokens, x_cols = z.shape
    groups = c_conv.shape[1] // STATE
    width = x_cols // groups
    heads = width // HEAD_DIM
    blocks = tokens // SPAN
    return pl.pallas_call(
        carry_kernel,
        grid=(groups,),
        in_specs=[
            pl.BlockSpec((width, STATE), lambda g: (g, 0)),
            pl.BlockSpec((blocks, width, STATE), lambda g: (0, g, 0)),
            pl.BlockSpec((tokens, STATE), lambda g: (0, g)),
            pl.BlockSpec((heads, tokens), lambda g: (g, 0)),
            pl.BlockSpec((blocks, width, SPAN), lambda g: (0, g, 0)),
            pl.BlockSpec((tokens, width), lambda g: (0, g)),
            pl.BlockSpec((1, width), lambda g: (0, g)),
        ],
        out_specs=pl.BlockSpec((tokens, width), lambda g: (0, g)),
        out_shape=jax.ShapeDtypeStruct((tokens, x_cols), jnp.bfloat16),
        scratch_shapes=[
            pltpu.VMEM((width, STATE), jnp.float32),
            pltpu.VMEM((width, SPAN), jnp.float32),
        ],
        compiler_params=pltpu.CompilerParams(dimension_semantics=("arbitrary",)),
        cost_estimate=pl.CostEstimate(
            flops=5000000000, bytes_accessed=14000000, transcendentals=1000000
        ),
        name="carry_norm",
    )(start, pieces, c_conv, cum_t, y_t, z, gain[None])


def prefix_kernel(count, final_ref, logs_ref, out_ref, pieces, logs, starts, *sems):
    piece_send, piece_recv, log_send, log_recv, start_send, start_recv, own = sems
    seq = lax.axis_index("seq")
    head = lax.axis_index("head")
    rows = pieces.shape[1]
    barrier = pltpu.get_barrier_semaphore()

    def peer_of(step):
        return lax.rem(seq + step, count)

    def part(which):
        return pl.ds(pl.multiple_of(which * rows, 16), rows)

    def remote(source, target, send, recv, peer):
        return pltpu.make_async_remote_copy(
            src_ref=source,
            dst_ref=target,
            send_sem=send,
            recv_sem=recv,
            device_id=(peer, head),
            device_id_type=pl.DeviceIdType.MESH,
        )

    def log_copy(step):
        return remote(
            logs_ref, logs.at[seq], log_send.at[step], log_recv.at[step], peer_of(step)
        )

    def piece_copy(step):
        return remote(
            final_ref.at[part(peer_of(step))],
            pieces.at[seq],
            piece_send.at[step],
            piece_recv.at[step],
            peer_of(step),
        )

    def start_copy(step):
        return remote(
            starts.at[peer_of(step)],
            out_ref.at[part(seq)],
            start_send.at[step],
            start_recv.at[step],
            peer_of(step),
        )

    def each(body):
        def lap(step, carry):
            body(step)
            return carry

        lax.fori_loop(1, count, lap, 0)

    def greet(step):
        pl.semaphore_signal(
            barrier, inc=1, device_id=(peer_of(step), head), device_id_type=pl.DeviceIdType.MESH
        )

    each(greet)
    pl.semaphore_wait(barrier, count - 1)

    def send(step):
        log_copy(step).start()
        piece_copy(step).start()

    each(send)
    own_piece = pltpu.make_async_copy(final_ref.at[part(seq)], pieces.at[seq], own.at[0])
    own_log = pltpu.make_async_copy(logs_ref, logs.at[seq], own.at[1])
    own_piece.start()
    own_log.start()
    own_piece.wait()
    own_log.wait()

    def land(step):
        log_copy(step).wait()
        piece_copy(step).wait()

    each(land)
    per_head = min(rows, HEAD_DIM)
    first = seq * rows // HEAD_DIM
    lanes = logs.shape[2]

    def scan(position, running):
        for index in range(rows // per_head):
            low = index * per_head
            starts[position, low : low + per_head, :] = running[index].astype(jnp.bfloat16)
        decays = jnp.exp(pltpu.roll(logs[position], lax.rem(lanes - first, lanes), 1))
        following = []
        for index in range(rows // per_head):
            low = index * per_head
            piece = pieces[position, low : low + per_head, :].astype(jnp.float32)
            following.append(decays[0:1, index : index + 1] * running[index] + piece)
        return tuple(following)

    zero = jnp.zeros((per_head, pieces.shape[2]), jnp.float32)
    lax.fori_loop(0, count, scan, (zero,) * (rows // per_head))
    each(lambda step: start_copy(step).start())
    own_start = pltpu.make_async_copy(starts.at[seq], out_ref.at[part(seq)], own.at[0])
    own_start.start()
    own_start.wait()
    each(lambda step: start_copy(step).wait())


def carry_in(log_total, final_state):
    count = lax.axis_size("seq")
    total, width = final_state.shape
    rows = total // count
    logs = jnp.broadcast_to(jnp.pad(log_total, (0, 128 - log_total.shape[0]))[None], (8, 128))
    vmem = pl.BlockSpec(memory_space=pltpu.VMEM)
    dma = pltpu.SemaphoreType.DMA
    return pl.pallas_call(
        functools.partial(prefix_kernel, count),
        out_shape=jax.ShapeDtypeStruct(final_state.shape, final_state.dtype),
        in_specs=[vmem, vmem],
        out_specs=vmem,
        scratch_shapes=[
            pltpu.VMEM((count, rows, width), jnp.bfloat16),
            pltpu.VMEM((count, 8, 128), jnp.float32),
            pltpu.VMEM((count, rows, width), jnp.bfloat16),
            dma((count,)),
            dma((count,)),
            dma((count,)),
            dma((count,)),
            dma((count,)),
            dma((count,)),
            dma((2,)),
        ],
        compiler_params=pltpu.CompilerParams(collective_id=1, has_side_effects=True),
        name="prefix_exchange",
    )(final_state, logs)


def project_kernel(
    heads, normed, weight, out, buffer, terms, landed, load_sems, send_sems, recv_sems
):
    seq = lax.axis_index("seq")
    head = lax.axis_index("head")
    rows = out.shape[0]
    tile = buffer.shape[2]
    tiles = out.shape[1] // tile
    barrier = pltpu.get_barrier_semaphore()
    for step in range(1, heads):
        pl.semaphore_signal(
            barrier,
            inc=1,
            device_id=(seq, lax.rem(head + step, heads)),
            device_id_type=pl.DeviceIdType.MESH,
        )
    pl.semaphore_wait(barrier, heads - 1)

    def load(index):
        slot = lax.rem(index, 2)
        return pltpu.make_async_copy(
            weight.at[index],
            buffer.at[slot],
            load_sems.at[slot],
        )

    def share(index, step):
        peer = lax.rem(head + step, heads)
        return pltpu.make_async_remote_copy(
            src_ref=terms.at[index, pl.ds(pl.multiple_of(peer * rows, 16), rows)],
            dst_ref=landed.at[index, step - 1],
            send_sem=send_sems.at[index, step - 1],
            recv_sem=recv_sems.at[index, step - 1],
            device_id=(seq, peer),
            device_id_type=pl.DeviceIdType.MESH,
        )

    load(0).start()

    def multiply(index, carry):
        @pl.when(index + 1 < tiles)
        def _():
            load(index + 1).start()

        load(index).wait()
        product = jnp.dot(
            normed[...], buffer[lax.rem(index, 2)], preferred_element_type=jnp.float32
        )
        terms[index] = product.astype(jnp.bfloat16)
        for step in range(1, heads):
            share(index, step).start()
        return carry

    lax.fori_loop(0, tiles, multiply, 0)
    for index in range(tiles):
        own = terms[index, pl.ds(pl.multiple_of(head * rows, 16), rows), :]
        total = own.astype(jnp.float32)
        for step in range(1, heads):
            share(index, step).wait()
            total = total + landed[index, step - 1].astype(jnp.float32)
        out[:, index * tile : (index + 1) * tile] = total.astype(jnp.bfloat16)


def project(normed, weight):
    heads = lax.axis_size("head")
    tokens, depth = normed.shape
    tiles, _, tile = weight.shape
    columns = tiles * tile
    rows = tokens // heads
    dma = pltpu.SemaphoreType.DMA
    return pl.pallas_call(
        functools.partial(project_kernel, heads),
        out_shape=jax.ShapeDtypeStruct((rows, columns), jnp.bfloat16),
        in_specs=[
            pl.BlockSpec(memory_space=pltpu.VMEM),
            pl.BlockSpec(memory_space=pl.ANY),
        ],
        out_specs=pl.BlockSpec(memory_space=pltpu.VMEM),
        scratch_shapes=[
            pltpu.VMEM((2, depth, tile), jnp.bfloat16),
            pltpu.VMEM((tiles, tokens, tile), jnp.bfloat16),
            pltpu.VMEM((tiles, heads - 1, rows, tile), jnp.bfloat16),
            dma((2,)),
            dma((tiles, heads - 1)),
            dma((tiles, heads - 1)),
        ],
        compiler_params=pltpu.CompilerParams(collective_id=2, has_side_effects=True),
        cost_estimate=pl.CostEstimate(
            flops=2 * tokens * depth * columns,
            bytes_accessed=2 * depth * columns,
            transcendentals=0,
        ),
        name="project",
    )(normed, weight)


def per_device(
    x_proj,
    z_proj,
    b_proj,
    c_proj,
    dt_raw,
    dt_bias,
    a_log,
    d_skip,
    conv_x,
    conv_bias_x,
    conv_bc,
    conv_bias_bc,
    norm_weight,
    out_weight,
):
    x_heads, z_heads, b_heads, c_heads, dt_full, *halos = entry_exchange(
        x_proj, z_proj, b_proj, c_proj, dt_raw
    )
    token_count = x_heads.shape[0]
    local_heads = dt_bias.shape[0]
    local_groups = b_heads.shape[1] // STATE
    per_group = local_heads // local_groups
    blocks = token_count // SPAN
    dt_heads = lax.dynamic_slice_in_dim(
        dt_full, lax.axis_index("head") * local_heads, local_heads, axis=1
    )
    step_size = jax.nn.softplus(dt_heads.astype(jnp.float32) + dt_bias)
    rate = (-jnp.exp(a_log) * step_size).reshape(blocks, SPAN, local_heads)
    cumulative = jnp.cumsum(rate, axis=1)
    log_total = jnp.sum(cumulative[:, -1], axis=0)
    cumulative = cumulative.reshape(token_count, local_heads)
    step_t = step_size.T
    cum_t = cumulative.T
    cum_c = jnp.transpose(
        cumulative.reshape(token_count, local_groups, per_group), (1, 0, 2)
    )
    y_t, pieces, final_state, c_conv = local_scan(
        x_heads,
        b_heads,
        c_heads,
        halos,
        conv_x,
        conv_bias_x,
        conv_bc,
        conv_bias_bc,
        step_t,
        cum_t,
        cum_c,
        d_skip.reshape(local_groups, per_group, 1),
    )
    start = carry_in(log_total, final_state)
    normed = carry_norm(start, pieces, c_conv, cum_t, y_t, z_heads, norm_weight)
    weight = lax.all_gather(out_weight, "seq")
    return project(normed, weight)


def solution(mesh):
    in_specs = (
        P(("seq", "head"), None),
        P(("seq", "head"), None),
        P(("seq", "head"), None),
        P(("seq", "head"), None),
        P(("seq", "head"), None),
        P("head"),
        P("head"),
        P("head"),
        P(None, "head"),
        P("head"),
        P(None, None, "head"),
        P(None, "head"),
        P("head"),
        P("head", "seq"),
    )
    out_specs = P(("seq", "head"), None)
    return jax.shard_map(
        per_device, mesh=mesh, in_specs=in_specs, out_specs=out_specs, check_vma=False
    )
```

profile of v0, /device:TPU:17, one launch (start us, length us, event | category | flops | bytes accessed | tf_op | source)
XLA Modules:
  0.0 262.5 jit_solution(12688132750508319992)
XLA Ops:
  6.5 0.0 all-gather.3.cloned.1.call-start
  6.5 0.7 all-gather.3.cloned.1.call-update
  7.3 0.0 copy-start.4
  7.3 0.0 copy-start.2
  7.3 0.0 copy-start.3
  7.3 0.0 copy-start.1
  7.3 0.0 copy-start
  7.3 75.8 %entry_exchange.1 = (bf16[256,4096]{1,0:T(8,128)(2,1)}, bf16[256,4096]{1,0:T(8,128)(2,1)}, bf16[256,512]{1,0:T(8,128)(2,1)}, bf16[256,512]{1,0:T(8,128)(2,1)}, b...) custom-call(bf16[128,8192]{1,0:T(8,128)(2,1)} %refs_0_.1, ...), custom_call_target="tpu_custom_call" | custom-call | tf_op jit(solution)/shard_map/entry_exchange/pallas_call | solution.py:143
  83.1 0.9 copy.23
  84.1 0.0 copy-done.4
  84.1 0.0 copy-done.2
  84.1 0.7 fusion
  84.9 0.1 copy.29
  85.0 0.2 reduce_window_sum.11
  85.2 0.1 copy.25
  85.2 0.1 reshape_reshape.3
  85.3 0.6 copy.36
  85.9 1.0 copy.27
  87.0 0.0 copy-done.3
  87.0 0.8 reshape.16.skip_ref
  87.7 0.0 copy-done.1
  87.7 0.6 fusion.3
  88.3 0.0 copy-done
  88.4 0.6 copy_bitcast_fusion
  89.0 12.0 %local_scan.1 = (f32[2,4096,128]{2,1,0:T(8,128)}, f32[2,4096,128]{2,1,0:T(8,128)}, bf16[4096,128]{1,0:T(8,128)(2,1)}, bf16[256,512]{1,0:T(8,128)(2,1)}) custom-call(bf16[256,4096]{1,0:T(8,128)(2,1)} %get-tuple-element.17.x_ref, bf16[256,512]{1,0:T(8,128)(2,1)} %get-tuple-element.18.b_ref, bf16[256,512]{1,0:T(8,128)(2,1)} %get-tuple-element.19.c_ref, ...), custom_call_target="tpu_custom_call" | custom-call | flops 20000000000 | bytes 16000000 | tf_op jit(solution)/shard_map/local_scan/pallas_call | solution.py:283
  101.0 0.6 broadcast_in_dim.7.logs_ref
  101.6 79.7 %prefix_exchange.1.start_ref = bf16[4096,128]{1,0:T(8,128)(2,1)} custom-call(bf16[4096,128]{1,0:T(8,128)(2,1)} %get-tuple-element.24.final_ref, f32[8,128]{1,0:T(8,128)} %broadcast_in_dim.7.logs_ref), custom_call_target="tpu_custom_call" | custom-call | tf_op jit(solution)/shard_map/prefix_exchange/pallas_call | solution.py:488
  181.3 7.6 %carry_norm.1.normed = bf16[256,4096]{1,0:T(8,128)(2,1)} custom-call(bf16[4096,128]{1,0:T(8,128)(2,1)} %prefix_exchange.1.start_ref, f32[2,4096,128]{2,1,0:T(8,128)} %get-tuple-element.25.piece_ref, bf16[256,512]{1,0:T(8,128)(2,1)} %get-tuple-element.26.c_ref, f32[64,256]{1,0:T(8,128)} %bitcast.27, f32[2,4096,128]{2,1,0:T(8,128)} %get-tuple-element.27.y_ref, ...), custom_call_target="tpu_custom_call" | custom-call | flops 5000000000 | bytes 14000000 | tf_op jit(solution)/shard_map/carry_norm/pallas_call | solution.py:352
  189.0 34.6 %all-gather.3.cloned.1.call-done = bf16[65536,256]{1,0:T(8,128)(2,1)} async-done(((bf16[4096,256]{1,0:T(8,128)(2,1)}), bf16[65536,256]{1,0:T(8,128)(2,1)}) %all-gather.3.cloned.1.call-update) | async-done | bytes 33554448 | tf_op jit(solution)/shard_map/all_gather | solution.py:659
  223.5 29.9 %project.1 = bf16[128,4096]{1,0:T(8,128)(2,1)} custom-call(bf16[256,4096]{1,0:T(8,128)(2,1)} %carry_norm.1.normed, bf16[16,4096,256]{2,1,0:T(8,128)(2,1)} %bitcast.22), custom_call_target="tpu_custom_call" | custom-call | flops 8589934592 | bytes 33554432 | tf_op jit(solution)/shard_map/project/pallas_call | solution.py:580
  253.4 2.3 copy.38
  (4 shorter events, 0.0 us)
Async XLA Ops:
  6.5 217.0 %all-gather.3.cloned.1.call-start = ((), (), s32[]{:S(2)}) async-start(), calls=%async_computation | async-start | bytes 35651584 | tf_op jit(solution)/shard_map/all_gather | solution.py:659
  7.3 76.8 %copy-start.4 = (f32[64]{0:T(128)S(1)}, f32[64]{0:T(128)}, u32[]{:S(2)}) copy-start(f32[64]{0:T(128)} %param.20) | copy-start | bytes 772
  7.3 76.8 %copy-start.2 = (f32[64]{0:T(128)S(1)}, f32[64]{0:T(128)}, u32[]{:S(2)}) copy-start(f32[64]{0:T(128)} %param.19) | copy-start | bytes 772
  7.3 79.7 %copy-start.3 = (f32[64]{0:T(128)S(1)}, f32[64]{0:T(128)}, u32[]{:S(2)}) copy-start(f32[64]{0:T(128)} %param.21) | copy-start | bytes 772
  7.3 80.5 %copy-start.1 = (f32[2,512]{1,0:T(2,128)S(1)}, f32[2,512]{1,0:T(2,128)}, u32[]{:S(2)}) copy-start(f32[2,512]{1,0:T(2,128)} %param.25) | copy-start | bytes 12292
  7.3 81.0 %copy-start = (f32[4,2,512]{2,1,0:T(2,128)S(1)}, f32[4,2,512]{2,1,0:T(2,128)}, u32[]{:S(2)}) copy-start(f32[4,2,512]{2,1,0:T(2,128)} %param.24) | copy-start | bytes 49156
Sparse Core Ops, SparseCore 0:
  8.9 214.5 all-gather.2
where the time goes:
time: 265 us; the launch traced here: 263 us
  Pallas kernels  205 us (77%)
  waiting for transfers between devices  35.3 us (13%)
  between operations  13.5 us (5%)
  local copies, waits for them, and re-layouts  7.71 us (3%)
    pallas_call x1, Pallas kernels, carry_in(): pl.pallas_call(functools.partial(prefix_kernel, count), out_shape=jax.Sha...  79.7 us
    pallas_call x1, Pallas kernels, entry_exchange(): pl.pallas_call(functools.partial(entry_kernel, count, heads), out_shape=[...  75.8 us
    all_gather x1, waiting for transfers between devices, per_device(): weight = lax.all_gather(out_weight, 'seq')  34.6 us
    pallas_call x1, Pallas kernels, project(): pl.pallas_call(functools.partial(project_kernel, heads), out_shape=jax.Sh...  29.9 us
    pallas_call x1, Pallas kernels, local_scan(): pl.pallas_call(local_kernel, grid=(groups,), in_specs=in_specs, out_specs...  12 us
    pallas_call x1, Pallas kernels, carry_norm(): pl.pallas_call(carry_kernel, grid=(groups,), in_specs=[pl.BlockSpec((widt...  7.64 us
  transfers between devices with their start and end apart: 1, of which 1 were waited for; matrix products, arithmetic and copies ran while one was open for 2% of the time, Pallas kernels for 67%

commit v1 on v0

v1 whole, which is shorter than its diff:
```python
import functools
import types

import jax
import jax.numpy as jnp
from jax import lax
from jax.experimental import pallas as pl
from jax.experimental.pallas import tpu as pltpu
from jax.sharding import PartitionSpec as P

HEAD_DIM = 64
STATE = 128
SPAN = 128
HALO = 16
INNER = 4
CHUNKS = 16
STEPS = 8
AHEAD = 3
LANES = 128
NT = (((1,), (1,)), ((), ()))
MESH = pl.DeviceIdType.MESH


def relay_passes(outer):
    passes = 0
    for level in range(outer):
        room = outer - 1 - level
        behind = level // 2 + 1
        if room >= 1:
            passes = max(passes, behind * min(room, 2))
    return passes


def column_order(outer):
    evens = list(range(0, outer, 2))
    odds = list(range(1, outer, 2))
    return evens + odds


def conv_silu(value, halo, taps_of, bias, padded, dtype):
    tokens = value.shape[0]
    padded[0:8, :] = halo.astype(jnp.float32)
    padded[8 : 8 + tokens, :] = value.astype(jnp.float32)
    total = bias + jnp.zeros(value.shape, jnp.float32)
    taps = len(taps_of)
    for offset in range(taps):
        low = 8 - (taps - 1) + offset
        total = total + taps_of[offset] * padded[low : low + tokens, :]
    return (total / (1.0 + jnp.exp(-total))).astype(dtype)


def mixer_kernel(count, heads, names, *refs):
    r = types.SimpleNamespace(**dict(zip(names, refs)))
    seq = lax.axis_index("seq")
    head = lax.axis_index("head")
    outer = count // INNER
    inner = lax.rem(seq, INNER)
    level = lax.div(seq, INNER)
    rows = r.x_in.shape[0]
    tokens = rows * heads
    groups, _, width = r.x_buf.shape
    per = width // HEAD_DIM
    blocks = tokens // SPAN
    local_heads = groups * per
    part = width // INNER
    part_heads = part // HEAD_DIM
    depth = r.wv.shape[1]
    tile = r.wv.shape[2]
    chunk_rows = depth // CHUNKS
    step_rows = depth // STEPS
    passes = relay_passes(outer)
    taps = r.conv_x.shape[0]
    dtype = r.x_buf.dtype

    near = seq + 1 - 2 * lax.rem(seq, 2)
    side = seq + 2 - 4 * lax.rem(lax.div(seq, 2), 2)
    cross = near + side - seq
    mates = (seq, near, side, cross)
    inners = tuple(lax.rem(mate, INNER) for mate in mates)

    def remote(source, target, send, recv, device):
        return pltpu.make_async_remote_copy(
            src_ref=source,
            dst_ref=target,
            send_sem=send,
            recv_sem=recv,
            device_id=device,
            device_id_type=MESH,
        )

    def head_of(step):
        return lax.rem(head + step, heads)

    barrier = pltpu.get_barrier_semaphore()
    gives_halo = jnp.logical_and(head == heads - 1, seq < count - 1)
    takes_halo = seq > 0
    gives_out = jnp.logical_and(gives_halo, inner == INNER - 1)
    takes_out = jnp.logical_and(takes_halo, inner == 0)

    def greet(where, which):
        pl.semaphore_signal(barrier, inc=1, device_id=(where, which), device_id_type=MESH)

    for index, mate in enumerate(mates):
        for step in range(heads):
            if index or step:
                greet(mate, head_of(step))
    expected = jnp.int32(INNER * heads - 1)
    for sign in (1, -1):
        for distance in (1, 2):
            there = level + sign * distance
            exists = jnp.logical_and(there >= 0, there < outer)

            @pl.when(exists)
            def _(there=there):
                greet(there * INNER + inner, head)

            expected = expected + jnp.where(exists, 1, 0)

    @pl.when(gives_out)
    def _():
        for which in range(heads):
            greet(seq + 1, which)

    @pl.when(takes_out)
    def _():
        greet(seq - 1, heads - 1)

    expected = expected + jnp.where(gives_out, heads, 0) + jnp.where(takes_out, 1, 0)
    pl.semaphore_wait(barrier, expected)

    mine = pl.ds(pl.multiple_of(head * rows, 16), rows)
    plan = (
        (r.b_in, r.b_buf, STATE),
        (r.c_in, r.c_buf, STATE),
        (r.x_in, r.x_buf, width),
        (r.z_in, r.z_buf, width),
    )
    halos = ((r.x_in, r.x_halo), (r.b_in, r.b_halo), (r.c_in, r.c_halo))

    def halo_copy(index, which, device):
        source, target = halos[index]
        size = target.shape[1]
        return remote(
            source.at[pl.ds(rows - HALO, HALO), pl.ds(which * size, size)],
            target,
            r.halo_send.at[index, which],
            r.halo_recv.at[index],
            device,
        )

    def entry_view(kind, which, g):
        source, target, size = plan[kind]
        low = pl.multiple_of((which * groups + g) * size, LANES)
        return source.at[:, pl.ds(low, size)], target.at[g, mine]

    def entry_copy(kind, g, step):
        source, target = entry_view(kind, head_of(step), g)
        return remote(
            source,
            target,
            r.entry_send.at[kind, step, g],
            r.entry_recv.at[kind, step, g],
            (seq, head_of(step)),
        )

    def own_copy(kind, g):
        source, target = entry_view(kind, head, g)
        return pltpu.make_async_copy(source, target, r.own_sems.at[kind, g])

    def dt_copy(step):
        return remote(
            r.dt_in,
            r.dt_buf.at[mine],
            r.dt_send.at[step],
            r.dt_recv.at[step],
            (seq, head_of(step)),
        )

    own_dt = pltpu.make_async_copy(r.dt_in, r.dt_buf.at[mine], r.misc_sems.at[0])
    own_weight = pltpu.make_async_copy(r.w_in, r.wv.at[level], r.misc_sems.at[1])

    own_dt.start()
    for step in range(1, heads):
        dt_copy(step).start()
    own_weight.start()

    @pl.when(gives_halo)
    def _():
        for index in range(len(halos)):
            for which in range(heads):
                halo_copy(index, which, (seq + 1, which)).start()

    for g in range(groups):
        for kind in range(3):
            own_copy(kind, g).start()
            for step in range(1, heads):
                entry_copy(kind, g, step).start()
    for g in range(groups):
        own_copy(3, g).start()
        for step in range(1, heads):
            entry_copy(3, g, step).start()

    def weight_item(sign, which, chunk, act):
        room = outer - 1 - level if sign > 0 else level
        behind = lax.div(level if sign > 0 else outer - 1 - level, 2)
        far = room >= 2
        hops = jnp.where(far, lax.div(which, 2), which)
        distance = jnp.where(far, 2 - lax.rem(which, 2), 1)
        exists = jnp.logical_and(room >= 1, hops <= behind)
        block = level - sign * 2 * hops
        target = (level + sign * distance) * INNER + inner
        view = r.wv.at[block, pl.ds(pl.multiple_of(chunk * chunk_rows, 16), chunk_rows)]
        copy = remote(
            view,
            view,
            r.weight_send.at[0 if sign > 0 else 1, which, chunk],
            r.weight_recv.at[block, chunk],
            (target, head),
        )
        if act == "wait":

            @pl.when(exists)
            def _():
                copy.wait_send()

            return
        fresh = jnp.logical_or(jnp.logical_not(far), distance == 2)
        relayed = jnp.logical_and(jnp.logical_and(exists, hops >= 1), fresh)

        @pl.when(relayed)
        def _():
            copy.wait_recv()

        @pl.when(exists)
        def _():
            copy.start()

    def weight_pass(which, chunk):
        if passes:
            weight_item(1, which, chunk, "start")
            weight_item(-1, which, chunk, "start")

    def weight_arrived(block, chunk):
        below = block < level
        apart = jnp.where(below, level - block, block - level)
        room = jnp.where(below, outer - 1 - level, level)
        relayed = jnp.logical_and(lax.rem(apart, 2) == 0, room >= 1)

        @pl.when(jnp.logical_and(apart > 0, jnp.logical_not(relayed)))
        def _():
            view = r.wv.at[block, pl.ds(pl.multiple_of(chunk * chunk_rows, 16), chunk_rows)]
            remote(
                view,
                view,
                r.weight_send.at[0, 0, chunk],
                r.weight_recv.at[block, chunk],
                (seq, head),
            ).wait_recv()

    own_weight.wait()
    for chunk in range(AHEAD):
        weight_pass(0, chunk)

    r.params[...] = jnp.zeros_like(r.params)
    r.params[0:1, 0:local_heads] = r.dt_bias[...]
    r.params[1:2, 0:local_heads] = r.a_log[...]
    columns = r.params[...].T
    bias = columns[0:local_heads, 0:1]
    coeff = -jnp.exp(columns[0:local_heads, 1:2])
    own_dt.wait()
    for step in range(1, heads):
        dt_copy(step).wait_recv()
    early = lax.broadcasted_iota(jnp.int32, (SPAN, SPAN), 0)
    late = lax.broadcasted_iota(jnp.int32, (SPAN, SPAN), 1)
    prefix_ones = jnp.where(early <= late, 1.0, 0.0).astype(jnp.float32)
    r.cum_pad[...] = jnp.zeros_like(r.cum_pad)
    log_total = jnp.zeros((1, LANES), jnp.float32)
    for block in range(blocks):
        span = slice(block * SPAN, (block + 1) * SPAN)
        r.dt_t[...] = r.dt_buf[span, :].astype(jnp.float32).T
        raw = r.dt_t[pl.ds(pl.multiple_of(head * local_heads, 8), local_heads), :] + bias
        step_size = jnp.maximum(raw, 0.0) + jnp.log1p(jnp.exp(-jnp.abs(raw)))
        r.step_t[:, span] = step_size
        summed = jnp.dot(
            coeff * step_size,
            prefix_ones,
            preferred_element_type=jnp.float32,
            precision=lax.Precision.HIGHEST,
        )
        r.cum_t[:, span] = summed
        r.cum_pad[0:local_heads, :] = summed
        by_token = r.cum_pad[...].T
        log_total = log_total + by_token[SPAN - 1 : SPAN, :]
        for g in range(groups):
            shift = (LANES - g * per) % LANES
            r.cum_c[g, span, :] = pltpu.roll(by_token, shift, 1) if shift else by_token
    logs = jnp.broadcast_to(log_total, (8, LANES))
    r.log_out[...] = logs
    r.log_in[inner] = logs

    def log_copy(index):
        return remote(
            r.log_out,
            r.log_in.at[inner],
            r.log_send.at[index],
            r.log_recv.at[index],
            (mates[index], head),
        )

    for index in range(1, INNER):
        log_copy(index).start()

    @pl.when(jnp.logical_not(takes_halo))
    def _():
        for _, target in halos:
            target[...] = jnp.zeros_like(target)

    @pl.when(takes_halo)
    def _():
        for index in range(len(halos)):
            halo_copy(index, 0, (seq, head)).wait_recv()

    @pl.when(level == 0)
    def _():
        r.chain_in[...] = jnp.zeros_like(r.chain_in)

    causal = early >= late

    def piece_copy(g, index):
        low = pl.multiple_of(inners[index] * part, 16)
        return remote(
            r.final_out.at[g, pl.ds(low, part)],
            r.piece_in.at[g, inner],
            r.piece_send.at[g, index],
            r.piece_recv.at[g, index],
            (mates[index], head),
        )

    def local(g, carry):
        for kind in range(3):
            own_copy(kind, g).wait()
            for step in range(1, heads):
                entry_copy(kind, g, step).wait_recv()
        wide = pl.ds(pl.multiple_of(g * width, LANES), width)
        slim = pl.ds(pl.multiple_of(g * STATE, LANES), STATE)
        x_conv = conv_silu(
            r.x_buf[g],
            r.x_halo[HALO - 8 : HALO, wide],
            [r.conv_x[tap : tap + 1, wide] for tap in range(taps)],
            r.bias_x[:, wide],
            r.x_pad,
            dtype,
        )
        b_conv = conv_silu(
            r.b_buf[g],
            r.b_halo[HALO - 8 : HALO, slim],
            [r.conv_bc[tap, 0:1, slim] for tap in range(taps)],
            r.bias_bc[0:1, slim],
            r.bc_pad,
            dtype,
        )
        c_conv = conv_silu(
            r.c_buf[g],
            r.c_halo[HALO - 8 : HALO, slim],
            [r.conv_bc[tap, 1:2, slim] for tap in range(taps)],
            r.bias_bc[1:2, slim],
            r.bc_pad,
            dtype,
        )
        r.c_conv[g] = c_conv
        own_heads = pl.ds(pl.multiple_of(g * per, 8), per)
        for block in range(blocks):
            low = block * SPAN
            b_blk = b_conv[low : low + SPAN]
            c_blk = c_conv[low : low + SPAN]
            r.x_t[...] = x_conv[low : low + SPAN].astype(jnp.float32).T
            scores = lax.dot_general(c_blk, b_blk, NT, preferred_element_type=jnp.float32)
            cum_rows = r.cum_t[own_heads, low : low + SPAN]
            step_all = r.step_t[own_heads, low : low + SPAN]
            for index in range(per):
                lines = pl.ds(index * HEAD_DIM, HEAD_DIM)
                column = r.cum_c[g, low : low + SPAN, index : index + 1]
                row = cum_rows[index : index + 1, :]
                step = step_all[index : index + 1, :]
                total = row[:, SPAN - 1 : SPAN]
                decays = jnp.exp(jnp.where(causal, column - row, -jnp.inf))
                mix = (decays * step * scores).astype(dtype)
                x_head = r.x_t[lines, :]
                product = lax.dot_general(
                    x_head.astype(dtype), mix, NT, preferred_element_type=jnp.float32
                )
                r.y_t[g, block, lines, :] = product + r.skip[g * per + index] * x_head
                r.x_w[lines, :] = (x_head * (step * jnp.exp(total - row))).astype(dtype)
            piece = jnp.dot(r.x_w[...], b_blk, preferred_element_type=jnp.float32)
            if block < blocks - 1:
                r.pieces[g, block] = piece
            if block == 0:
                r.final[...] = piece
            else:
                r.running[...] = piece
                for index in range(per):
                    lines = pl.ds(index * HEAD_DIM, HEAD_DIM)
                    decay = jnp.exp(cum_rows[index : index + 1, SPAN - 1 : SPAN])
                    r.final[lines, :] = decay * r.final[lines, :] + r.running[lines, :]
        r.final_out[g] = r.final[...].astype(dtype)
        for index in range(1, INNER):
            piece_copy(g, index).start()
        own_part = pl.ds(pl.multiple_of(inner * part, 16), part)
        r.piece_in[g, inner] = r.final_out[g, own_part, :]
        weight_pass(0, AHEAD + g)
        return carry

    lax.fori_loop(0, groups, local, 0)

    def chain_copy(g, where):
        return remote(
            r.chain_out.at[g],
            r.chain_in.at[g],
            r.chain_send.at[g],
            r.chain_recv.at[g],
            (where, head),
        )

    def start_copy(g, index):
        low = pl.multiple_of(inner * part, 16)
        return remote(
            r.start_out.at[g, inners[index]],
            r.start_in.at[g, pl.ds(low, part)],
            r.start_send.at[g, index],
            r.start_recv.at[g, index],
            (mates[index], head),
        )

    for index in range(1, INNER):
        log_copy(index).wait_recv()

    def carry_step(g, carry):
        for index in range(1, INNER):
            piece_copy(g, index).wait_recv()

        @pl.when(level > 0)
        def _():
            chain_copy(g, seq).wait_recv()

        first = g * per + inner * part_heads
        state = [
            r.chain_in[g, index * HEAD_DIM : (index + 1) * HEAD_DIM, :].astype(jnp.float32)
            for index in range(part_heads)
        ]
        for position in range(INNER):
            decays = jnp.exp(pltpu.roll(r.log_in[position], lax.rem(LANES - first, LANES), 1))
            for index in range(part_heads):
                lines = slice(index * HEAD_DIM, (index + 1) * HEAD_DIM)
                r.start_out[g, position, lines, :] = state[index].astype(dtype)
                piece = r.piece_in[g, position, lines, :].astype(jnp.float32)
                state[index] = decays[0:1, index : index + 1] * state[index] + piece
        for index in range(part_heads):
            r.chain_out[g, index * HEAD_DIM : (index + 1) * HEAD_DIM, :] = state[index].astype(
                dtype
            )

        @pl.when(level < outer - 1)
        def _():
            chain_copy(g, seq + INNER).start()

        for index in range(1, INNER):
            start_copy(g, index).start()
        own_part = pl.ds(pl.multiple_of(inner * part, 16), part)
        r.start_in[g, own_part, :] = r.start_out[g, inner]
        weight_pass(0, AHEAD + groups + g)
        return carry

    lax.fori_loop(0, groups, carry_step, 0)

    def share_copy(g, index):
        target = r.a_buf.at[g, pl.ds(index * tokens, tokens)]
        return remote(
            r.a_buf.at[g, pl.ds(0, tokens)],
            target,
            r.share_send.at[g, index],
            r.share_recv.at[g, index],
            (mates[index], head),
        )

    def forward_copy(g):
        return remote(
            r.a_buf.at[g, pl.ds(2 * tokens, tokens)],
            r.a_buf.at[g, pl.ds(3 * tokens, tokens)],
            r.share_send.at[g, 3],
            r.share_recv.at[g, 3],
            (near, head),
        )

    def norm_step(g, carry):
        for index in range(1, INNER):
            start_copy(g, index).wait_recv()
        own_copy(3, g).wait()
        for step in range(1, heads):
            entry_copy(3, g, step).wait_recv()
        wide = pl.ds(pl.multiple_of(g * width, LANES), width)
        own_heads = pl.ds(pl.multiple_of(g * per, 8), per)
        r.running[...] = r.start_in[g].astype(jnp.float32)
        for block in range(blocks):
            low = block * SPAN
            c_blk = r.c_conv[g, low : low + SPAN, :]
            r.x_t[...] = lax.dot_general(
                r.running[...].astype(dtype), c_blk, NT, preferred_element_type=jnp.float32
            )
            grown = jnp.exp(r.cum_t[own_heads, low : low + SPAN])
            for index in range(per):
                lines = pl.ds(index * HEAD_DIM, HEAD_DIM)
                row = grown[index : index + 1, :]
                r.x_t[lines, :] = r.y_t[g, block, lines, :] + r.x_t[lines, :] * row
                if block < blocks - 1:
                    r.running[lines, :] = (
                        row[:, SPAN - 1 : SPAN] * r.running[lines, :]
                        + r.pieces[g, block, lines, :]
                    )
            gate = r.z_buf[g, low : low + SPAN, :].astype(jnp.float32)
            gated = r.x_t[...].T * (gate / (1.0 + jnp.exp(-gate)))
            mean = jnp.sum(gated * gated, axis=-1, keepdims=True) * (1.0 / width)
            normed = gated * lax.rsqrt(mean + 1.0)
            r.a_buf[g, low : low + SPAN, :] = (normed * r.gain[:, wide]).astype(dtype)
        share_copy(g, 2).start()
        share_copy(g, 1).start()
        weight_pass(0, AHEAD + 2 * groups + g)
        return carry

    lax.fori_loop(0, groups, norm_step, 0)

    def rest(which, low):
        def body(chunk, carry):
            weight_pass(which, chunk)
            return carry

        lax.fori_loop(low, CHUNKS, body, 0)

    rest(0, min(AHEAD + 3 * groups, CHUNKS))

    def later_pass(which, carry):
        rest(which, 0)
        return carry

    if passes > 1:
        lax.fori_loop(1, passes, later_pass, 0)

    order = column_order(outer)
    early_count = (outer + 1) // 2
    direction = jnp.where(level < (outer + 1) // 2, 1, -1)

    def block_at(index):
        return lax.rem(level + direction * order[index] + outer, outer)

    steps_per_group = width // step_rows

    def product(block, step, low, size):
        g = lax.div(step, steps_per_group)
        off = pl.multiple_of(lax.rem(step, steps_per_group) * step_rows, LANES)
        down = pl.multiple_of(step * step_rows, 16)
        return jnp.dot(
            r.a_buf[g, low : low + size, pl.ds(off, step_rows)],
            r.wv[block, pl.ds(down, step_rows), :],
            preferred_element_type=jnp.float32,
        )

    per_step = CHUNKS // STEPS

    def arrive(block, step):
        for extra in range(per_step):
            weight_arrived(block, step * per_step + extra)

    def result_copy(index, mate, which):
        low = pl.multiple_of(mate * tokens + which * rows, 16)
        return remote(
            r.terms.at[index, pl.ds(low, rows)],
            r.landed.at[head, block_at(index) * INNER + inner],
            r.term_send.at[index, mate, which],
            r.term_recv.at[head, block_at(index) * INNER + inner],
            (mates[mate], which),
        )

    def ship(index, low_mate, mate_count):
        for mate in range(low_mate, low_mate + mate_count):
            for which in range(heads):
                if mate == 0:

                    @pl.when(head != which)
                    def _(mate=mate, which=which):
                        result_copy(index, mate, which).start()

                else:
                    result_copy(index, mate, which).start()
        if low_mate == 0:
            own_rows = pl.ds(pl.multiple_of(head * rows, 16), rows)
            r.landed[head, block_at(index) * INNER + inner] = r.terms[index, own_rows, :]

    half = 2 * tokens

    def unit(index, low, waits):
        block = block_at(index)
        r.acc[0, 0:half, :] = jnp.zeros((half, tile), jnp.float32)

        def body(step, carry):
            if waits:
                arrive(block, step)
            r.acc[0, 0:half, :] += product(block, step, low, half)
            return carry

        lax.fori_loop(0, STEPS, body, 0)
        r.terms[index, low : low + half, :] = r.acc[0, 0:half, :].astype(dtype)

    for g in range(groups):
        share_copy(g, 1).wait_recv()
    for index in range(early_count):
        unit(index, 0, True)
        ship(index, 0, 2)

    def pass_on(g, carry):
        share_copy(g, 2).wait_recv()
        forward_copy(g).start()
        return carry

    lax.fori_loop(0, groups, pass_on, 0)

    def passed(g, carry):
        forward_copy(g).wait_recv()
        return carry

    lax.fori_loop(0, groups, passed, 0)
    for index in range(early_count):
        unit(index, half, False)
        ship(index, 2, 2)

    late_indices = list(range(early_count, outer))
    if late_indices:
        r.acc[...] = jnp.zeros_like(r.acc)

        def late_step(step, carry):
            for slot, index in enumerate(late_indices):
                block = block_at(index)
                arrive(block, step)
                r.acc[slot] += product(block, step, 0, 2 * half)
            return carry

        lax.fori_loop(0, STEPS, late_step, 0)
        for slot, index in enumerate(late_indices):
            r.terms[index] = r.acc[slot].astype(dtype)
            ship(index, 2, 2)
            ship(index, 0, 2)

    for position in range(count):
        for which in range(heads):
            local_one = jnp.logical_and(which == head, lax.rem(position, INNER) == inner)

            @pl.when(jnp.logical_not(local_one))
            def _(which=which, position=position):
                remote(
                    r.terms.at[0, pl.ds(0, rows)],
                    r.landed.at[which, position],
                    r.term_send.at[0, 0, 0],
                    r.term_recv.at[which, position],
                    (seq, head),
                ).wait_recv()

    for position in range(count):
        total = r.landed[0, position].astype(jnp.float32)
        for which in range(1, heads):
            total = total + r.landed[which, position].astype(jnp.float32)
        r.out[:, position * tile : (position + 1) * tile] = total.astype(dtype)

    @pl.when(gives_halo)
    def _():
        for index in range(len(halos)):
            for which in range(heads):
                halo_copy(index, which, (seq + 1, which)).wait_send()

    for step in range(1, heads):
        dt_copy(step).wait_send()
    for index in range(1, INNER):
        log_copy(index).wait_send()

    def drain(g, carry):
        for kind in range(4):
            for step in range(1, heads):
                entry_copy(kind, g, step).wait_send()
        for index in range(1, INNER):
            piece_copy(g, index).wait_send()
            start_copy(g, index).wait_send()

        @pl.when(level < outer - 1)
        def _():
            chain_copy(g, seq).wait_send()

        share_copy(g, 1).wait_send()
        share_copy(g, 2).wait_send()
        forward_copy(g).wait_send()
        return carry

    lax.fori_loop(0, groups, drain, 0)
    if passes:

        def drain_weight(item, carry):
            which = lax.div(item, CHUNKS)
            chunk = lax.rem(item, CHUNKS)
            weight_item(1, which, chunk, "wait")
            weight_item(-1, which, chunk, "wait")
            return carry

        lax.fori_loop(0, passes * CHUNKS, drain_weight, 0)
    for index in range(outer):
        for mate in range(INNER):
            for which in range(heads):
                if mate == 0:

                    @pl.when(head != which)
                    def _(index=index, which=which):
                        result_copy(index, 0, which).wait_send()

                else:
                    result_copy(index, mate, which).wait_send()


def per_device(
    x_proj,
    z_proj,
    b_proj,
    c_proj,
    dt_raw,
    dt_bias,
    a_log,
    d_skip,
    conv_x,
    conv_bias_x,
    conv_bc,
    conv_bias_bc,
    norm_weight,
    out_weight,
):
    count = lax.axis_size("seq")
    heads = lax.axis_size("head")
    outer = count // INNER
    rows = x_proj.shape[0]
    tokens = rows * heads
    cols = x_proj.shape[1] // heads
    groups = b_proj.shape[1] // heads // STATE
    width = cols // groups
    local_heads = dt_bias.shape[0]
    blocks = tokens // SPAN
    part = width // INNER
    depth, tile = out_weight.shape
    passes = max(relay_passes(outer), 1)
    late = max(outer - (outer + 1) // 2, 1)
    dtype = x_proj.dtype
    f32 = jnp.float32
    vmem = pl.BlockSpec(memory_space=pltpu.VMEM)
    smem = pl.BlockSpec(memory_space=pltpu.SMEM)
    hbm = pl.BlockSpec(memory_space=pl.ANY)
    dma = pltpu.SemaphoreType.DMA
    inputs = {
        "x_in": (x_proj, hbm),
        "z_in": (z_proj, hbm),
        "b_in": (b_proj, hbm),
        "c_in": (c_proj, hbm),
        "dt_in": (dt_raw, hbm),
        "w_in": (out_weight, hbm),
        "dt_bias": (dt_bias[None], vmem),
        "a_log": (a_log[None], vmem),
        "skip": (d_skip, smem),
        "conv_x": (conv_x, vmem),
        "bias_x": (conv_bias_x[None], vmem),
        "conv_bc": (conv_bc, vmem),
        "bias_bc": (conv_bias_bc, vmem),
        "gain": (norm_weight[None], vmem),
    }
    scratch = {
        "x_buf": pltpu.VMEM((groups, tokens, width), dtype),
        "z_buf": pltpu.VMEM((groups, tokens, width), dtype),
        "b_buf": pltpu.VMEM((groups, tokens, STATE), dtype),
        "c_buf": pltpu.VMEM((groups, tokens, STATE), dtype),
        "dt_buf": pltpu.VMEM((tokens, dt_raw.shape[1]), dtype),
        "x_halo": pltpu.VMEM((HALO, cols), dtype),
        "b_halo": pltpu.VMEM((HALO, groups * STATE), dtype),
        "c_halo": pltpu.VMEM((HALO, groups * STATE), dtype),
        "wv": pltpu.VMEM((outer, depth, tile), dtype),
        "params": pltpu.VMEM((LANES, LANES), f32),
        "dt_t": pltpu.VMEM((dt_raw.shape[1], SPAN), f32),
        "step_t": pltpu.VMEM((local_heads, tokens), f32),
        "cum_t": pltpu.VMEM((local_heads, tokens), f32),
        "cum_pad": pltpu.VMEM((LANES, SPAN), f32),
        "cum_c": pltpu.VMEM((groups, tokens, LANES), f32),
        "log_out": pltpu.VMEM((8, LANES), f32),
        "log_in": pltpu.VMEM((INNER, 8, LANES), f32),
        "x_pad": pltpu.VMEM((tokens + 8, width), f32),
        "bc_pad": pltpu.VMEM((tokens + 8, STATE), f32),
        "x_t": pltpu.VMEM((width, SPAN), f32),
        "x_w": pltpu.VMEM((width, SPAN), dtype),
        "c_conv": pltpu.VMEM((groups, tokens, STATE), dtype),
        "y_t": pltpu.VMEM((groups, blocks, width, SPAN), f32),
        "pieces": pltpu.VMEM((groups, max(blocks - 1, 1), width, STATE), f32),
        "final": pltpu.VMEM((width, STATE), f32),
        "running": pltpu.VMEM((width, STATE), f32),
        "final_out": pltpu.VMEM((groups, width, STATE), dtype),
        "piece_in": pltpu.VMEM((groups, INNER, part, STATE), dtype),
        "chain_in": pltpu.VMEM((groups, part, STATE), dtype),
        "chain_out": pltpu.VMEM((groups, part, STATE), dtype),
        "start_out": pltpu.VMEM((groups, INNER, part, STATE), dtype),
        "start_in": pltpu.VMEM((groups, width, STATE), dtype),
        "a_buf": pltpu.VMEM((groups, INNER * tokens, width), dtype),
        "acc": pltpu.VMEM((late, INNER * tokens, tile), f32),
        "terms": pltpu.VMEM((outer, INNER * tokens, tile), dtype),
        "landed": pltpu.VMEM((heads, count, rows, tile), dtype),
        "entry_send": dma((4, heads, groups)),
        "entry_recv": dma((4, heads, groups)),
        "own_sems": dma((4, groups)),
        "misc_sems": dma((2,)),
        "dt_send": dma((heads,)),
        "dt_recv": dma((heads,)),
        "halo_send": dma((3, heads)),
        "halo_recv": dma((3,)),
        "weight_send": dma((2, passes, CHUNKS)),
        "weight_recv": dma((outer, CHUNKS)),
        "log_send": dma((INNER,)),
        "log_recv": dma((INNER,)),
        "piece_send": dma((groups, INNER)),
        "piece_recv": dma((groups, INNER)),
        "chain_send": dma((groups,)),
        "chain_recv": dma((groups,)),
        "start_send": dma((groups, INNER)),
        "start_recv": dma((groups, INNER)),
        "share_send": dma((groups, INNER)),
        "share_recv": dma((groups, INNER)),
        "term_send": dma((outer, INNER, heads)),
        "term_recv": dma((heads, count)),
    }
    names = list(inputs) + ["out"] + list(scratch)
    return pl.pallas_call(
        functools.partial(mixer_kernel, count, heads, names),
        out_shape=jax.ShapeDtypeStruct((rows, count * tile), dtype),
        in_specs=[spec for _, spec in inputs.values()],
        out_specs=vmem,
        scratch_shapes=list(scratch.values()),
        compiler_params=pltpu.CompilerParams(
            collective_id=0, has_side_effects=True, vmem_limit_bytes=60 * 1024 * 1024
        ),
        name="mixer",
    )(*[value for value, _ in inputs.values()])


def solution(mesh):
    in_specs = (
        P(("seq", "head"), None),
        P(("seq", "head"), None),
        P(("seq", "head"), None),
        P(("seq", "head"), None),
        P(("seq", "head"), None),
        P("head"),
        P("head"),
        P("head"),
        P(None, "head"),
        P("head"),
        P(None, None, "head"),
        P(None, "head"),
        P("head"),
        P("head", "seq"),
    )
    out_specs = P(("seq", "head"), None)
    return jax.shard_map(
        per_device, mesh=mesh, in_specs=in_specs, out_specs=out_specs, check_vma=False
    )
```

time: 265 us -> 203 us (0.77)
  waiting for transfers between devices: 35.3 us -> 0 us
  between operations: 13.5 us -> 0.01 us
  Pallas kernels: 205 us -> 198 us
  local copies, waits for them, and re-layouts: 7.71 us -> 2.29 us
    all_gather x1 -> x0, waiting for transfers between devices: 34.6 us -> none  [per_device(): weight = lax.all_gather(out_weight, 'seq')]
    pallas_call x5 -> x1, Pallas kernels: 205 us -> 198 us  [per_device(): pl.pallas_call(functools.partial(mixer_kernel, count, heads, names), out_...]
  transfers between devices with their start and end apart: 1 -> 0, of which waited for: 1 -> 0; matrix products, arithmetic and copies ran while one was open for 2% -> 0% of each run, Pallas kernels for 67% -> 0%
where the time goes in v1:
time: 203 us; the launch traced here: 200 us
  Pallas kernels  198 us (98%)
  local copies, waits for them, and re-layouts  2.29 us (1%)
    pallas_call x1, Pallas kernels, per_device(): pl.pallas_call(functools.partial(mixer_kernel, count, heads, names), out_...  198 us

profile of v1, /device:TPU:17, one launch (start us, length us, event | category | flops | bytes accessed | tf_op | source)
XLA Modules:
  0.0 200.3 jit_solution(2010811546456999963)
XLA Ops:
  0.0 198.0 %mixer.1 = bf16[128,4096]{1,0:T(8,128)(2,1)} custom-call(bf16[128,8192]{1,0:T(8,128)(2,1)} %refs_0_.1, bf16[128,8192]{1,0:T(8,128)(2,1)} %refs_1_.1, bf16[128,1024]{1,0:T(8,128)(2,1)} %refs_2_.1, bf16[128,1024]{1,0:T(8,128)(2,1)} %refs_3_.1, bf16[128,128]{1,0:T(8,128)(2,1)} %refs_4_.1, bf16[4096,256]{1,0:T(8,128)(2,1)} %refs_5_.1, f32[1,64]{1,0:T(1,128)} %bitcast.6, ...), custom_call_target="tpu_custom_call" | custom-call | tf_op jit(solution)/shard_map/mixer/pallas_call | solution.py:836
  198.0 2.3 %copy.16 = bf16[128,4096]{1,0:T(8,128)(2,1)} copy(bf16[128,4096]{1,0:T(8,128)(2,1)} %mixer.1) | data formatting | bytes 2097152

commit v2 on v1

--- a/solution.py
+++ b/solution.py
@@ -15,7 +15,10 @@
 INNER = 4
 CHUNKS = 16
 STEPS = 8
-AHEAD = 3
+OPENING = 2
+RELAYED = 4
+FIRST = 4
+LATE_GROUP = 3
 LANES = 128
 NT = (((1,), (1,)), ((), ()))
 MESH = pl.DeviceIdType.MESH
@@ -31,10 +34,12 @@
     return passes
 
 
-def column_order(outer):
-    evens = list(range(0, outer, 2))
-    odds = list(range(1, outer, 2))
-    return evens + odds
+def column_orders(outer):
+    edge = list(range(outer))
+    if outer < 4:
+        return edge, edge
+    first = [0, 2, outer - 1, 1]
+    return edge, first + [offset for offset in edge if offset not in first]
 
 
 def conv_silu(value, halo, taps_of, bias, padded, dtype):
@@ -126,7 +131,8 @@
         greet(seq - 1, heads - 1)
 
     expected = expected + jnp.where(gives_out, heads, 0) + jnp.where(takes_out, 1, 0)
-    pl.semaphore_wait(barrier, expected)
+    with jax.named_scope("greeting"):
+        pl.semaphore_wait(barrier, expected)
 
     mine = pl.ds(pl.multiple_of(head * rows, 16), rows)
     plan = (
@@ -200,28 +206,46 @@
         for step in range(1, heads):
             entry_copy(3, g, step).start()
 
-    def weight_item(sign, which, chunk, act):
+    def weight_item(sign, which, chunk, kinds):
         room = outer - 1 - level if sign > 0 else level
         behind = lax.div(level if sign > 0 else outer - 1 - level, 2)
         far = room >= 2
         hops = jnp.where(far, lax.div(which, 2), which)
         distance = jnp.where(far, 2 - lax.rem(which, 2), 1)
         exists = jnp.logical_and(room >= 1, hops <= behind)
+        edge = level == 0 if sign > 0 else level == outer - 1
+        if kinds is not None:
+            between = jnp.logical_and(far, jnp.logical_not(edge))
+            chosen = jnp.bool_(False)
+            if "edge" in kinds:
+                chosen = jnp.logical_or(chosen, jnp.logical_and(far, edge))
+            if "last" in kinds:
+                chosen = jnp.logical_or(chosen, jnp.logical_not(far))
+            if ("up" if sign > 0 else "down") in kinds:
+                chosen = jnp.logical_or(chosen, between)
+            exists = jnp.logical_and(exists, chosen)
         block = level - sign * 2 * hops
         target = (level + sign * distance) * INNER + inner
         view = r.wv.at[block, pl.ds(pl.multiple_of(chunk * chunk_rows, 16), chunk_rows)]
         copy = remote(
             view,
             view,
-            r.weight_send.at[0 if sign > 0 else 1, which, chunk],
+            r.weight_send.at[0 if sign > 0 else 1, which],
             r.weight_recv.at[block, chunk],
             (target, head),
         )
-        if act == "wait":
+        if kinds is None:
 
             @pl.when(exists)
             def _():
-                copy.wait_send()
+                whole = r.wv.at[level]
+                remote(
+                    whole,
+                    whole,
+                    r.weight_send.at[0 if sign > 0 else 1, which],
+                    r.weight_recv.at[level, 0],
+                    (target, head),
+                ).wait_send()
 
             return
         fresh = jnp.logical_or(jnp.logical_not(far), distance == 2)
@@ -235,10 +259,15 @@
         def _():
             copy.start()
 
-    def weight_pass(which, chunk):
-        if passes:
-            weight_item(1, which, chunk, "start")
-            weight_item(-1, which, chunk, "start")
+    def weight_pass(which, kinds, low=0, high=CHUNKS):
+        def body(chunk, carry):
+            if set(kinds) != {"down"}:
+                weight_item(1, which, chunk, kinds)
+            if set(kinds) != {"up"}:
+                weight_item(-1, which, chunk, kinds)
+            return carry
+
+        lax.fori_loop(low, high, body, 0)
 
     def weight_arrived(block, chunk):
         below = block < level
@@ -252,14 +281,16 @@
             remote(
                 view,
                 view,
-                r.weight_send.at[0, 0, chunk],
+                r.weight_send.at[0, 0],
                 r.weight_recv.at[block, chunk],
                 (seq, head),
             ).wait_recv()
 
     own_weight.wait()
-    for chunk in range(AHEAD):
-        weight_pass(0, chunk)
+    if passes > 1:
+        weight_pass(1, ("edge", "up"), 0, OPENING)
+    if passes:
+        weight_pass(0, ("edge", "last", "down"))
 
     r.params[...] = jnp.zeros_like(r.params)
     r.params[0:1, 0:local_heads] = r.dt_bias[...]
@@ -337,10 +368,11 @@
         )
 
     def local(g, carry):
-        for kind in range(3):
-            own_copy(kind, g).wait()
-            for step in range(1, heads):
-                entry_copy(kind, g, step).wait_recv()
+        with jax.named_scope("local_wait"):
+            for kind in range(3):
+                own_copy(kind, g).wait()
+                for step in range(1, heads):
+                    entry_copy(kind, g, step).wait_recv()
         wide = pl.ds(pl.multiple_of(g * width, LANES), width)
         slim = pl.ds(pl.multiple_of(g * STATE, LANES), STATE)
         x_conv = conv_silu(
@@ -407,10 +439,12 @@
             piece_copy(g, index).start()
         own_part = pl.ds(pl.multiple_of(inner * part, 16), part)
         r.piece_in[g, inner] = r.final_out[g, own_part, :]
-        weight_pass(0, AHEAD + g)
         return carry
 
-    lax.fori_loop(0, groups, local, 0)
+    with jax.named_scope("local_all"):
+        lax.fori_loop(0, groups, local, 0)
+    if passes > 1:
+        weight_pass(1, ("last",), 0, RELAYED)
 
     def chain_copy(g, where):
         return remote(
@@ -435,12 +469,13 @@
         log_copy(index).wait_recv()
 
     def carry_step(g, carry):
-        for index in range(1, INNER):
-            piece_copy(g, index).wait_recv()
-
-        @pl.when(level > 0)
-        def _():
-            chain_copy(g, seq).wait_recv()
+        with jax.named_scope("carry_wait"):
+            for index in range(1, INNER):
+                piece_copy(g, index).wait_recv()
+
+            @pl.when(level > 0)
+            def _():
+                chain_copy(g, seq).wait_recv()
 
         first = g * per + inner * part_heads
         state = [
@@ -467,10 +502,27 @@
             start_copy(g, index).start()
         own_part = pl.ds(pl.multiple_of(inner * part, 16), part)
         r.start_in[g, own_part, :] = r.start_out[g, inner]
-        weight_pass(0, AHEAD + groups + g)
         return carry
 
-    lax.fori_loop(0, groups, carry_step, 0)
+    with jax.named_scope("carry_all"):
+        lax.fori_loop(0, groups, carry_step, 0)
+
+    def chain_left(g, carry):
+        @pl.when(level < outer - 1)
+        def _():
+            chain_copy(g, seq).wait_send()
+
+        return carry
+
+    with jax.named_scope("chain_left"):
+        lax.fori_loop(0, groups, chain_left, 0)
+
+    if passes > 1:
+        with jax.named_scope("pass_one_early"):
+            weight_pass(1, ("edge",), OPENING)
+            weight_pass(1, ("last",), RELAYED)
+            weight_pass(1, ("down",))
+            weight_pass(1, ("up",), OPENING, OPENING + FIRST)
 
     def share_copy(g, index):
         target = r.a_buf.at[g, pl.ds(index * tokens, tokens)]
@@ -492,11 +544,12 @@
         )
 
     def norm_step(g, carry):
-        for index in range(1, INNER):
-            start_copy(g, index).wait_recv()
-        own_copy(3, g).wait()
-        for step in range(1, heads):
-            entry_copy(3, g, step).wait_recv()
+        with jax.named_scope("norm_wait"):
+            for index in range(1, INNER):
+                start_copy(g, index).wait_recv()
+            own_copy(3, g).wait()
+            for step in range(1, heads):
+                entry_copy(3, g, step).wait_recv()
         wide = pl.ds(pl.multiple_of(g * width, LANES), width)
         own_heads = pl.ds(pl.multiple_of(g * per, 8), per)
         r.running[...] = r.start_in[g].astype(jnp.float32)
@@ -523,33 +576,37 @@
             r.a_buf[g, low : low + SPAN, :] = (normed * r.gain[:, wide]).astype(dtype)
         share_copy(g, 2).start()
         share_copy(g, 1).start()
-        weight_pass(0, AHEAD + 2 * groups + g)
+
+        if passes:
+
+            @pl.when(g == min(LATE_GROUP, groups - 1))
+            def _():
+                weight_pass(0, ("up",))
+
         return carry
 
-    lax.fori_loop(0, groups, norm_step, 0)
-
-    def rest(which, low):
-        def body(chunk, carry):
-            weight_pass(which, chunk)
-            return carry
-
-        lax.fori_loop(low, CHUNKS, body, 0)
-
-    rest(0, min(AHEAD + 3 * groups, CHUNKS))
+    with jax.named_scope("norm_all"):
+        lax.fori_loop(0, groups, norm_step, 0)
+
+    if passes > 1:
+        with jax.named_scope("pass_one_late"):
+            weight_pass(1, ("up",), OPENING + FIRST)
 
     def later_pass(which, carry):
-        rest(which, 0)
+        weight_pass(which, ("edge", "last", "up", "down"))
         return carry
 
-    if passes > 1:
-        lax.fori_loop(1, passes, later_pass, 0)
-
-    order = column_order(outer)
-    early_count = (outer + 1) // 2
+    if passes > 2:
+        lax.fori_loop(2, passes, later_pass, 0)
+
+    edge_order, inner_order = column_orders(outer)
+    early_count = min(2, outer)
+    at_edge = jnp.logical_or(level == 0, level == outer - 1)
     direction = jnp.where(level < (outer + 1) // 2, 1, -1)
 
     def block_at(index):
-        return lax.rem(level + direction * order[index] + outer, outer)
+        offset = jnp.where(at_edge, edge_order[index], inner_order[index])
+        return lax.rem(level + direction * offset + outer, outer)
 
     steps_per_group = width // step_rows
 
@@ -574,7 +631,7 @@
         return remote(
             r.terms.at[index, pl.ds(low, rows)],
             r.landed.at[head, block_at(index) * INNER + inner],
-            r.term_send.at[index, mate, which],
+            r.term_send.at[index],
             r.term_recv.at[head, block_at(index) * INNER + inner],
             (mates[mate], which),
         )
@@ -596,77 +653,44 @@
 
     half = 2 * tokens
 
-    def unit(index, low, waits):
+    def unit(index, low, size, waits):
         block = block_at(index)
-        r.acc[0, 0:half, :] = jnp.zeros((half, tile), jnp.float32)
+        r.acc[0:size, :] = jnp.zeros((size, tile), jnp.float32)
 
         def body(step, carry):
             if waits:
                 arrive(block, step)
-            r.acc[0, 0:half, :] += product(block, step, low, half)
+            r.acc[0:size, :] += product(block, step, low, size)
             return carry
 
         lax.fori_loop(0, STEPS, body, 0)
-        r.terms[index, low : low + half, :] = r.acc[0, 0:half, :].astype(dtype)
+        r.terms[index, low : low + size, :] = r.acc[0:size, :].astype(dtype)
 
     for g in range(groups):
         share_copy(g, 1).wait_recv()
     for index in range(early_count):
-        unit(index, 0, True)
-        ship(index, 0, 2)
+        with jax.named_scope("early_zero"):
+            unit(index, 0, half, True)
+            ship(index, 0, 2)
 
     def pass_on(g, carry):
         share_copy(g, 2).wait_recv()
         forward_copy(g).start()
         return carry
 
-    lax.fori_loop(0, groups, pass_on, 0)
+    with jax.named_scope("pass_on"):
+        lax.fori_loop(0, groups, pass_on, 0)
 
     def passed(g, carry):
         forward_copy(g).wait_recv()
         return carry
 
-    lax.fori_loop(0, groups, passed, 0)
+    with jax.named_scope("passed"):
+        lax.fori_loop(0, groups, passed, 0)
     for index in range(early_count):
-        unit(index, half, False)
-        ship(index, 2, 2)
-
-    late_indices = list(range(early_count, outer))
-    if late_indices:
-        r.acc[...] = jnp.zeros_like(r.acc)
-
-        def late_step(step, carry):
-            for slot, index in enumerate(late_indices):
-                block = block_at(index)
-                arrive(block, step)
-                r.acc[slot] += product(block, step, 0, 2 * half)
-            return carry
-
-        lax.fori_loop(0, STEPS, late_step, 0)
-        for slot, index in enumerate(late_indices):
-            r.terms[index] = r.acc[slot].astype(dtype)
+        with jax.named_scope("early_one"):
+            unit(index, half, half, False)
             ship(index, 2, 2)
-            ship(index, 0, 2)
-
-    for position in range(count):
-        for which in range(heads):
-            local_one = jnp.logical_and(which == head, lax.rem(position, INNER) == inner)
-
-            @pl.when(jnp.logical_not(local_one))
-            def _(which=which, position=position):
-                remote(
-                    r.terms.at[0, pl.ds(0, rows)],
-                    r.landed.at[which, position],
-                    r.term_send.at[0, 0, 0],
-                    r.term_recv.at[which, position],
-                    (seq, head),
-                ).wait_recv()
-
-    for position in range(count):
-        total = r.landed[0, position].astype(jnp.float32)
-        for which in range(1, heads):
-            total = total + r.landed[which, position].astype(jnp.float32)
-        r.out[:, position * tile : (position + 1) * tile] = total.astype(dtype)
 
     @pl.when(gives_halo)
     def _():
@@ -686,38 +710,67 @@
         for index in range(1, INNER):
             piece_copy(g, index).wait_send()
             start_copy(g, index).wait_send()
-
-        @pl.when(level < outer - 1)
-        def _():
-            chain_copy(g, seq).wait_send()
-
         share_copy(g, 1).wait_send()
         share_copy(g, 2).wait_send()
         forward_copy(g).wait_send()
         return carry
 
     lax.fori_loop(0, groups, drain, 0)
-    if passes:
-
-        def drain_weight(item, carry):
-            which = lax.div(item, CHUNKS)
-            chunk = lax.rem(item, CHUNKS)
-            weight_item(1, which, chunk, "wait")
-            weight_item(-1, which, chunk, "wait")
-            return carry
-
-        lax.fori_loop(0, passes * CHUNKS, drain_weight, 0)
-    for index in range(outer):
+
+    def results_of(index):
         for mate in range(INNER):
             for which in range(heads):
-                if mate == 0:
-
-                    @pl.when(head != which)
-                    def _(index=index, which=which):
-                        result_copy(index, 0, which).wait_send()
-
-                else:
-                    result_copy(index, mate, which).wait_send()
+                position = block_at(index) * INNER + mate
+                local_one = jnp.logical_and(which == head, mate == inner)
+
+                @pl.when(jnp.logical_not(local_one))
+                def _(which=which, position=position):
+                    remote(
+                        r.terms.at[0, pl.ds(0, rows)],
+                        r.landed.at[which, position],
+                        r.term_send.at[0],
+                        r.term_recv.at[which, position],
+                        (near, head),
+                    ).wait_recv()
+
+    for index in range(early_count, outer):
+        if index == outer - 1:
+            with jax.named_scope("results_early"):
+                for before in range(index):
+                    results_of(before)
+        with jax.named_scope("late"):
+            unit(index, 0, 2 * half, True)
+            ship(index, 2, 2)
+            ship(index, 0, 2)
+
+    with jax.named_scope("result_wait"):
+        for index in range(0 if outer == early_count else outer - 1, outer):
+            results_of(index)
+
+    with jax.named_scope("assembly"):
+        for position in range(count):
+            total = r.landed[0, position].astype(jnp.float32)
+            for which in range(1, heads):
+                total = total + r.landed[which, position].astype(jnp.float32)
+            r.out[:, position * tile : (position + 1) * tile] = total.astype(dtype)
+
+    if passes:
+
+        def drain_weight(which, carry):
+            weight_item(1, which, 0, None)
+            weight_item(-1, which, 0, None)
+            return carry
+
+        lax.fori_loop(0, passes, drain_weight, 0)
+    for index in range(outer):
+        sent = pl.ds(0, (INNER * heads - 1) * rows)
+        remote(
+            r.terms.at[index, sent],
+            r.terms.at[index, sent],
+            r.term_send.at[index],
+            r.term_recv.at[0, 0],
+            (near, head),
+        ).wait_send()
 
 
 def per_device(
@@ -749,7 +802,6 @@
     part = width // INNER
     depth, tile = out_weight.shape
     passes = max(relay_passes(outer), 1)
-    late = max(outer - (outer + 1) // 2, 1)
     dtype = x_proj.dtype
     f32 = jnp.float32
     vmem = pl.BlockSpec(memory_space=pltpu.VMEM)
@@ -806,7 +858,7 @@
         "start_out": pltpu.VMEM((groups, INNER, part, STATE), dtype),
         "start_in": pltpu.VMEM((groups, width, STATE), dtype),
         "a_buf": pltpu.VMEM((groups, INNER * tokens, width), dtype),
-        "acc": pltpu.VMEM((late, INNER * tokens, tile), f32),
+        "acc": pltpu.VMEM((INNER * tokens, tile), f32),
         "terms": pltpu.VMEM((outer, INNER * tokens, tile), dtype),
         "landed": pltpu.VMEM((heads, count, rows, tile), dtype),
         "entry_send": dma((4, heads, groups)),
@@ -817,7 +869,7 @@
         "dt_recv": dma((heads,)),
         "halo_send": dma((3, heads)),
         "halo_recv": dma((3,)),
-        "weight_send": dma((2, passes, CHUNKS)),
+        "weight_send": dma((2, passes)),
         "weight_recv": dma((outer, CHUNKS)),
         "log_send": dma((INNER,)),
         "log_recv": dma((INNER,)),
@@ -829,7 +881,7 @@
         "start_recv": dma((groups, INNER)),
         "share_send": dma((groups, INNER)),
         "share_recv": dma((groups, INNER)),
-        "term_send": dma((outer, INNER, heads)),
+        "term_send": dma((outer,)),
         "term_recv": dma((heads, count)),
     }
     names = list(inputs) + ["out"] + list(scratch)

time: 203 us -> 168 us (0.83); the launches traced: 200 us -> 168 us
  Pallas kernels: 198 us -> 166 us
    pallas_call x1, Pallas kernels: 198 us -> 166 us  [per_device(): pl.pallas_call(functools.partial(mixer_kernel, count, heads, names), out_...]
where the time goes in v2:
time: 168 us
  Pallas kernels  166 us (99%)
  local copies, waits for them, and re-layouts  2.29 us (1%)
    pallas_call x1, Pallas kernels, per_device(): pl.pallas_call(functools.partial(mixer_kernel, count, heads, names), out_...  166 us

profile of v2, /device:TPU:17, one launch (start us, length us, event | category | flops | bytes accessed | tf_op | source)
XLA Modules:
  0.0 167.9 jit_solution(11364130698074877364)
XLA Ops:
  0.0 165.6 %mixer.1 = bf16[128,4096]{1,0:T(8,128)(2,1)} custom-call(bf16[128,8192]{1,0:T(8,128)(2,1)} %refs_0_.1, bf16[128,8192]{1,0:T(8,128)(2,1)} %refs_1_.1, bf16[128,1024]{1,0:T(8,128)(2,1)} %refs_2_.1, bf16[128,1024]{1,0:T(8,128)(2,1)} %refs_3_.1, bf16[128,128]{1,0:T(8,128)(2,1)} %refs_4_.1, bf16[4096,256]{1,0:T(8,128)(2,1)} %refs_5_.1, f32[1,64]{1,0:T(1,128)} %bitcast.6, ...), custom_call_target="tpu_custom_call" | custom-call | tf_op jit(solution)/shard_map/mixer/pallas_call | solution.py:888
  165.6 2.3 %copy.16 = bf16[128,4096]{1,0:T(8,128)(2,1)} copy(bf16[128,4096]{1,0:T(8,128)(2,1)} %mixer.1) | data formatting | bytes 2097152

commit v3 on v2

--- a/solution.py
+++ b/solution.py
@@ -16,6 +16,7 @@
 CHUNKS = 16
 STEPS = 8
 OPENING = 2
+BEFORE = 12
 RELAYED = 4
 FIRST = 4
 LATE_GROUP = 3
@@ -32,6 +33,10 @@
         if room >= 1:
             passes = max(passes, behind * min(room, 2))
     return passes
+
+
+def column_halves(tile):
+    return 2 if tile % (2 * LANES) == 0 else 1
 
 
 def column_orders(outer):
@@ -71,7 +76,10 @@
     part_heads = part // HEAD_DIM
     depth = r.wv.shape[1]
     tile = r.wv.shape[2]
-    chunk_rows = depth // CHUNKS
+    halves = column_halves(tile)
+    half_cols = tile // halves
+    per_half = CHUNKS // halves
+    chunk_rows = depth // per_half
     step_rows = depth // STEPS
     passes = relay_passes(outer)
     taps = r.conv_x.shape[0]
@@ -95,6 +103,12 @@
 
     def head_of(step):
         return lax.rem(head + step, heads)
+
+    def received(view, sem):
+        remote(view, view, r.spare.at[0], sem, (near, head)).wait_recv()
+
+    def sent(view, sem):
+        remote(view, view, sem, r.spare.at[0], (near, head)).wait_send()
 
     barrier = pltpu.get_barrier_semaphore()
     gives_halo = jnp.logical_and(head == heads - 1, seq < count - 1)
@@ -131,9 +145,6 @@
         greet(seq - 1, heads - 1)
 
     expected = expected + jnp.where(gives_out, heads, 0) + jnp.where(takes_out, 1, 0)
-    with jax.named_scope("greeting"):
-        pl.semaphore_wait(barrier, expected)
-
     mine = pl.ds(pl.multiple_of(head * rows, 16), rows)
     plan = (
         (r.b_in, r.b_buf, STATE),
@@ -164,8 +175,8 @@
         return remote(
             source,
             target,
-            r.entry_send.at[kind, step, g],
-            r.entry_recv.at[kind, step, g],
+            r.entry_send.at[kind, step - 1],
+            r.entry_recv.at[kind, step - 1, g],
             (seq, head_of(step)),
         )
 
@@ -185,10 +196,16 @@
     own_dt = pltpu.make_async_copy(r.dt_in, r.dt_buf.at[mine], r.misc_sems.at[0])
     own_weight = pltpu.make_async_copy(r.w_in, r.wv.at[level], r.misc_sems.at[1])
 
+    own_weight.start()
     own_dt.start()
+    for kind in range(4):
+        for g in range(groups):
+            own_copy(kind, g).start()
+    with jax.named_scope("greeting"):
+        pl.semaphore_wait(barrier, expected)
+
     for step in range(1, heads):
         dt_copy(step).start()
-    own_weight.start()
 
     @pl.when(gives_halo)
     def _():
@@ -196,15 +213,13 @@
             for which in range(heads):
                 halo_copy(index, which, (seq + 1, which)).start()
 
-    for g in range(groups):
-        for kind in range(3):
-            own_copy(kind, g).start()
-            for step in range(1, heads):
-                entry_copy(kind, g, step).start()
-    for g in range(groups):
-        own_copy(3, g).start()
-        for step in range(1, heads):
-            entry_copy(3, g, step).start()
+    def chunk_view(block, chunk):
+        low = pl.multiple_of(lax.rem(chunk, per_half) * chunk_rows, 16)
+        lines = pl.ds(low, chunk_rows)
+        if halves == 1:
+            return r.wv.at[block, lines]
+        left = pl.multiple_of(lax.div(chunk, per_half) * half_cols, LANES)
+        return r.wv.at[block, lines, pl.ds(left, half_cols)]
 
     def weight_item(sign, which, chunk, kinds):
         room = outer - 1 - level if sign > 0 else level
@@ -215,18 +230,18 @@
         exists = jnp.logical_and(room >= 1, hops <= behind)
         edge = level == 0 if sign > 0 else level == outer - 1
         if kinds is not None:
-            between = jnp.logical_and(far, jnp.logical_not(edge))
+            way = "up" if sign > 0 else "down"
             chosen = jnp.bool_(False)
-            if "edge" in kinds:
+            if "edge " + way in kinds:
                 chosen = jnp.logical_or(chosen, jnp.logical_and(far, edge))
-            if "last" in kinds:
+            if "last " + way in kinds:
                 chosen = jnp.logical_or(chosen, jnp.logical_not(far))
-            if ("up" if sign > 0 else "down") in kinds:
-                chosen = jnp.logical_or(chosen, between)
+            if "mid " + way in kinds:
+                chosen = jnp.logical_or(chosen, jnp.logical_and(far, jnp.logical_not(edge)))
             exists = jnp.logical_and(exists, chosen)
         block = level - sign * 2 * hops
         target = (level + sign * distance) * INNER + inner
-        view = r.wv.at[block, pl.ds(pl.multiple_of(chunk * chunk_rows, 16), chunk_rows)]
+        view = chunk_view(block, chunk)
         copy = remote(
             view,
             view,
@@ -261,10 +276,9 @@
 
     def weight_pass(which, kinds, low=0, high=CHUNKS):
         def body(chunk, carry):
-            if set(kinds) != {"down"}:
-                weight_item(1, which, chunk, kinds)
-            if set(kinds) != {"up"}:
-                weight_item(-1, which, chunk, kinds)
+            for sign, way in ((1, "up"), (-1, "down")):
+                if any(kind.endswith(way) for kind in kinds):
+                    weight_item(sign, which, chunk, kinds)
             return carry
 
         lax.fori_loop(low, high, body, 0)
@@ -277,7 +291,7 @@
 
         @pl.when(jnp.logical_and(apart > 0, jnp.logical_not(relayed)))
         def _():
-            view = r.wv.at[block, pl.ds(pl.multiple_of(chunk * chunk_rows, 16), chunk_rows)]
+            view = chunk_view(block, chunk)
             remote(
                 view,
                 view,
@@ -286,11 +300,23 @@
                 (seq, head),
             ).wait_recv()
 
+    for step in range(1, heads):
+        for kind in range(3):
+            entry_copy(kind, 0, step).start()
     own_weight.wait()
     if passes > 1:
-        weight_pass(1, ("edge", "up"), 0, OPENING)
+        weight_pass(1, ("edge up", "edge down", "mid up"), 0, OPENING)
     if passes:
-        weight_pass(0, ("edge", "last", "down"))
+        weight_pass(0, ("edge up", "edge down", "last up", "last down", "mid down"), 0, BEFORE)
+        weight_pass(0, ("edge down", "last up", "last down", "mid down"), BEFORE)
+
+    for g in range(1, groups):
+        for kind in range(3):
+            for step in range(1, heads):
+                entry_copy(kind, g, step).start()
+    for g in range(groups):
+        for step in range(1, heads):
+            entry_copy(3, g, step).start()
 
     r.params[...] = jnp.zeros_like(r.params)
     r.params[0:1, 0:local_heads] = r.dt_bias[...]
@@ -333,8 +359,8 @@
         return remote(
             r.log_out,
             r.log_in.at[inner],
-            r.log_send.at[index],
-            r.log_recv.at[index],
+            r.log_sems.at[0],
+            r.log_sems.at[1],
             (mates[index], head),
         )
 
@@ -362,8 +388,8 @@
         return remote(
             r.final_out.at[g, pl.ds(low, part)],
             r.piece_in.at[g, inner],
-            r.piece_send.at[g, index],
-            r.piece_recv.at[g, index],
+            r.piece_send.at[0],
+            r.piece_recv.at[g],
             (mates[index], head),
         )
 
@@ -444,13 +470,13 @@
     with jax.named_scope("local_all"):
         lax.fori_loop(0, groups, local, 0)
     if passes > 1:
-        weight_pass(1, ("last",), 0, RELAYED)
+        weight_pass(1, ("last down",), 0, RELAYED)
 
     def chain_copy(g, where):
         return remote(
             r.chain_out.at[g],
             r.chain_in.at[g],
-            r.chain_send.at[g],
+            r.chain_send.at[0],
             r.chain_recv.at[g],
             (where, head),
         )
@@ -460,18 +486,16 @@
         return remote(
             r.start_out.at[g, inners[index]],
             r.start_in.at[g, pl.ds(low, part)],
-            r.start_send.at[g, index],
-            r.start_recv.at[g, index],
+            r.start_send.at[0],
+            r.start_recv.at[g],
             (mates[index], head),
         )
 
-    for index in range(1, INNER):
-        log_copy(index).wait_recv()
+    received(r.log_in.at[1:INNER], r.log_sems.at[1])
 
     def carry_step(g, carry):
         with jax.named_scope("carry_wait"):
-            for index in range(1, INNER):
-                piece_copy(g, index).wait_recv()
+            received(r.piece_in.at[g, 1:INNER], r.piece_recv.at[g])
 
             @pl.when(level > 0)
             def _():
@@ -507,30 +531,27 @@
     with jax.named_scope("carry_all"):
         lax.fori_loop(0, groups, carry_step, 0)
 
-    def chain_left(g, carry):
+    with jax.named_scope("chain_left"):
+
         @pl.when(level < outer - 1)
         def _():
-            chain_copy(g, seq).wait_send()
-
-        return carry
-
-    with jax.named_scope("chain_left"):
-        lax.fori_loop(0, groups, chain_left, 0)
+            sent(r.chain_out, r.chain_send.at[0])
 
     if passes > 1:
         with jax.named_scope("pass_one_early"):
-            weight_pass(1, ("edge",), OPENING)
-            weight_pass(1, ("last",), RELAYED)
-            weight_pass(1, ("down",))
-            weight_pass(1, ("up",), OPENING, OPENING + FIRST)
+            weight_pass(1, ("edge up", "mid up"), OPENING, OPENING + FIRST)
+            weight_pass(1, ("edge down",), OPENING)
+            weight_pass(1, ("last down",), RELAYED)
+            weight_pass(1, ("mid down",))
+            weight_pass(1, ("last up",), 0, BEFORE)
 
     def share_copy(g, index):
         target = r.a_buf.at[g, pl.ds(index * tokens, tokens)]
         return remote(
             r.a_buf.at[g, pl.ds(0, tokens)],
             target,
-            r.share_send.at[g, index],
-            r.share_recv.at[g, index],
+            r.share_send.at[0],
+            r.share_recv.at[g] if index == 2 else r.near_recv.at[0],
             (mates[index], head),
         )
 
@@ -538,15 +559,14 @@
         return remote(
             r.a_buf.at[g, pl.ds(2 * tokens, tokens)],
             r.a_buf.at[g, pl.ds(3 * tokens, tokens)],
-            r.share_send.at[g, 3],
-            r.share_recv.at[g, 3],
+            r.share_send.at[0],
+            r.near_recv.at[1],
             (near, head),
         )
 
     def norm_step(g, carry):
         with jax.named_scope("norm_wait"):
-            for index in range(1, INNER):
-                start_copy(g, index).wait_recv()
+            received(r.start_in.at[g, pl.ds(0, (INNER - 1) * part)], r.start_recv.at[g])
             own_copy(3, g).wait()
             for step in range(1, heads):
                 entry_copy(3, g, step).wait_recv()
@@ -581,7 +601,8 @@
 
             @pl.when(g == min(LATE_GROUP, groups - 1))
             def _():
-                weight_pass(0, ("up",))
+                weight_pass(0, ("edge up",), BEFORE)
+                weight_pass(0, ("mid up",))
 
         return carry
 
@@ -590,10 +611,12 @@
 
     if passes > 1:
         with jax.named_scope("pass_one_late"):
-            weight_pass(1, ("up",), OPENING + FIRST)
+            weight_pass(1, ("edge up", "mid up"), OPENING + FIRST)
+            weight_pass(1, ("last up",), BEFORE)
 
     def later_pass(which, carry):
-        weight_pass(which, ("edge", "last", "up", "down"))
+        for part in ("edge", "last", "mid"):
+            weight_pass(which, (part + " up", part + " down"))
         return carry
 
     if passes > 2:
@@ -610,64 +633,68 @@
 
     steps_per_group = width // step_rows
 
-    def product(block, step, low, size):
+    def product(block, step, low, size, cols):
         g = lax.div(step, steps_per_group)
         off = pl.multiple_of(lax.rem(step, steps_per_group) * step_rows, LANES)
         down = pl.multiple_of(step * step_rows, 16)
         return jnp.dot(
             r.a_buf[g, low : low + size, pl.ds(off, step_rows)],
-            r.wv[block, pl.ds(down, step_rows), :],
+            r.wv[block, pl.ds(down, step_rows), cols],
             preferred_element_type=jnp.float32,
         )
 
-    per_step = CHUNKS // STEPS
-
-    def arrive(block, step):
-        for extra in range(per_step):
-            weight_arrived(block, step * per_step + extra)
-
-    def result_copy(index, mate, which):
+    per_step = per_half // STEPS
+    every = slice(0, tile)
+
+    def arrive(block, step, parts):
+        for which in parts:
+            for extra in range(per_step):
+                weight_arrived(block, which * per_half + step * per_step + extra)
+
+    def result_copy(index, mate, which, cols, slot):
         low = pl.multiple_of(mate * tokens + which * rows, 16)
+        spread = pl.ds(cols.start, cols.stop - cols.start)
+        position = block_at(index) * INNER + inner
         return remote(
-            r.terms.at[index, pl.ds(low, rows)],
-            r.landed.at[head, block_at(index) * INNER + inner],
-            r.term_send.at[index],
-            r.term_recv.at[head, block_at(index) * INNER + inner],
+            r.terms.at[index, pl.ds(low, rows), spread],
+            r.landed.at[head, position, :, spread],
+            r.term_send.at[index, slot],
+            r.term_recv.at[index, slot],
             (mates[mate], which),
         )
 
-    def ship(index, low_mate, mate_count):
+    def ship(index, low_mate, mate_count, cols=every, slot=0):
         for mate in range(low_mate, low_mate + mate_count):
             for which in range(heads):
                 if mate == 0:
 
                     @pl.when(head != which)
                     def _(mate=mate, which=which):
-                        result_copy(index, mate, which).start()
+                        result_copy(index, mate, which, cols, slot).start()
 
                 else:
-                    result_copy(index, mate, which).start()
+                    result_copy(index, mate, which, cols, slot).start()
         if low_mate == 0:
             own_rows = pl.ds(pl.multiple_of(head * rows, 16), rows)
-            r.landed[head, block_at(index) * INNER + inner] = r.terms[index, own_rows, :]
+            position = block_at(index) * INNER + inner
+            r.landed[head, position, :, cols] = r.terms[index, own_rows, cols]
 
     half = 2 * tokens
 
-    def unit(index, low, size, waits):
+    def unit(index, low, size, waits, cols=every, parts=tuple(range(halves))):
         block = block_at(index)
-        r.acc[0:size, :] = jnp.zeros((size, tile), jnp.float32)
+        r.acc[0:size, cols] = jnp.zeros((size, cols.stop - cols.start), jnp.float32)
 
         def body(step, carry):
             if waits:
-                arrive(block, step)
-            r.acc[0:size, :] += product(block, step, low, size)
+                arrive(block, step, parts)
+            r.acc[0:size, cols] += product(block, step, low, size, cols)
             return carry
 
         lax.fori_loop(0, STEPS, body, 0)
-        r.terms[index, low : low + size, :] = r.acc[0:size, :].astype(dtype)
-
-    for g in range(groups):
-        share_copy(g, 1).wait_recv()
+        r.terms[index, low : low + size, cols] = r.acc[0:size, cols].astype(dtype)
+
+    received(r.a_buf.at[:, pl.ds(tokens, tokens)], r.near_recv.at[0])
     for index in range(early_count):
         with jax.named_scope("early_zero"):
             unit(index, 0, half, True)
@@ -681,12 +708,8 @@
     with jax.named_scope("pass_on"):
         lax.fori_loop(0, groups, pass_on, 0)
 
-    def passed(g, carry):
-        forward_copy(g).wait_recv()
-        return carry
-
     with jax.named_scope("passed"):
-        lax.fori_loop(0, groups, passed, 0)
+        received(r.a_buf.at[:, pl.ds(3 * tokens, tokens)], r.near_recv.at[1])
     for index in range(early_count):
         with jax.named_scope("early_one"):
             unit(index, half, half, False)
@@ -700,77 +723,77 @@
 
     for step in range(1, heads):
         dt_copy(step).wait_send()
-    for index in range(1, INNER):
-        log_copy(index).wait_send()
-
-    def drain(g, carry):
-        for kind in range(4):
-            for step in range(1, heads):
-                entry_copy(kind, g, step).wait_send()
-        for index in range(1, INNER):
-            piece_copy(g, index).wait_send()
-            start_copy(g, index).wait_send()
-        share_copy(g, 1).wait_send()
-        share_copy(g, 2).wait_send()
-        forward_copy(g).wait_send()
-        return carry
-
-    lax.fori_loop(0, groups, drain, 0)
-
-    def results_of(index):
-        for mate in range(INNER):
-            for which in range(heads):
-                position = block_at(index) * INNER + mate
-                local_one = jnp.logical_and(which == head, mate == inner)
-
-                @pl.when(jnp.logical_not(local_one))
-                def _(which=which, position=position):
-                    remote(
-                        r.terms.at[0, pl.ds(0, rows)],
-                        r.landed.at[which, position],
-                        r.term_send.at[0],
-                        r.term_recv.at[which, position],
-                        (near, head),
-                    ).wait_recv()
+    sent(r.log_in.at[1:INNER], r.log_sems.at[0])
+
+    for kind, buffer in enumerate((r.b_buf, r.c_buf, r.x_buf, r.z_buf)):
+        for step in range(1, heads):
+            sent(buffer.at[:, mine], r.entry_send.at[kind, step - 1])
+    sent(r.piece_in.at[:, 1:INNER], r.piece_send.at[0])
+    sent(r.start_out.at[:, 1:INNER], r.start_send.at[0])
+    sent(r.a_buf.at[:, pl.ds(0, 3 * tokens)], r.share_send.at[0])
+
+    def parts_of(index):
+        if index < outer - 1 or index < early_count:
+            return [every]
+        return [slice(which * half_cols, (which + 1) * half_cols) for which in range(halves)]
+
+    def terms_view(index, cols):
+        lines = pl.ds(0, (INNER * heads - 1) * rows)
+        return r.terms.at[index, lines, pl.ds(cols.start, cols.stop - cols.start)]
+
+    def results_of(index, slot, cols):
+        received(terms_view(index, cols), r.term_recv.at[index, slot])
 
     for index in range(early_count, outer):
-        if index == outer - 1:
-            with jax.named_scope("results_early"):
-                for before in range(index):
-                    results_of(before)
-        with jax.named_scope("late"):
-            unit(index, 0, 2 * half, True)
-            ship(index, 2, 2)
-            ship(index, 0, 2)
-
-    with jax.named_scope("result_wait"):
-        for index in range(0 if outer == early_count else outer - 1, outer):
-            results_of(index)
-
-    with jax.named_scope("assembly"):
-        for position in range(count):
+        parts = parts_of(index)
+        for slot, cols in enumerate(parts):
+            with jax.named_scope("late"):
+                which = tuple(range(halves)) if len(parts) == 1 else (slot,)
+                unit(index, 0, 2 * half, True, cols, which)
+                ship(index, 2, 2, cols, slot)
+                ship(index, 0, 2, cols, slot)
+
+    spread = INNER * tile
+
+    def result_out(block):
+        where = pl.ds(block * spread, spread)
+        return pltpu.make_async_copy(r.stage.at[:, where], r.out.at[:, where], r.misc_sems.at[2])
+
+    def assemble(block):
+        for position in range(block * INNER, (block + 1) * INNER):
             total = r.landed[0, position].astype(jnp.float32)
             for which in range(1, heads):
                 total = total + r.landed[which, position].astype(jnp.float32)
-            r.out[:, position * tile : (position + 1) * tile] = total.astype(dtype)
-
-    if passes:
-
-        def drain_weight(which, carry):
-            weight_item(1, which, 0, None)
-            weight_item(-1, which, 0, None)
-            return carry
-
-        lax.fori_loop(0, passes, drain_weight, 0)
-    for index in range(outer):
-        sent = pl.ds(0, (INNER * heads - 1) * rows)
-        remote(
-            r.terms.at[index, sent],
-            r.terms.at[index, sent],
-            r.term_send.at[index],
-            r.term_recv.at[0, 0],
-            (near, head),
-        ).wait_send()
+            r.stage[:, position * tile : (position + 1) * tile] = total.astype(dtype)
+        result_out(block).start()
+
+    last_block = block_at(outer - 1)
+    with jax.named_scope("result_wait"):
+        for index in range(outer - 1):
+            results_of(index, 0, every)
+    with jax.named_scope("assembly"):
+        for block in range(outer):
+            pl.when(block != last_block)(functools.partial(assemble, block))
+    with jax.named_scope("result_wait_last"):
+        for slot, cols in enumerate(parts_of(outer - 1)):
+            results_of(outer - 1, slot, cols)
+    with jax.named_scope("assembly_last"):
+        for block in range(outer):
+            pl.when(block == last_block)(functools.partial(assemble, block))
+
+    with jax.named_scope("drain"):
+        pltpu.make_async_copy(r.stage, r.out, r.misc_sems.at[2]).wait()
+        if passes:
+
+            def drain_weight(which, carry):
+                weight_item(1, which, 0, None)
+                weight_item(-1, which, 0, None)
+                return carry
+
+            lax.fori_loop(0, passes, drain_weight, 0)
+        for index in range(outer):
+            for slot, cols in enumerate(parts_of(index)):
+                sent(terms_view(index, cols), r.term_send.at[index, slot])
 
 
 def per_device(
@@ -861,35 +884,37 @@
         "acc": pltpu.VMEM((INNER * tokens, tile), f32),
         "terms": pltpu.VMEM((outer, INNER * tokens, tile), dtype),
         "landed": pltpu.VMEM((heads, count, rows, tile), dtype),
-        "entry_send": dma((4, heads, groups)),
-        "entry_recv": dma((4, heads, groups)),
+        "entry_send": dma((4, max(heads - 1, 1))),
+        "entry_recv": dma((4, max(heads - 1, 1), groups)),
         "own_sems": dma((4, groups)),
-        "misc_sems": dma((2,)),
+        "stage": pltpu.VMEM((rows, count * tile), dtype),
+        "misc_sems": dma((3,)),
+        "spare": dma((1,)),
         "dt_send": dma((heads,)),
         "dt_recv": dma((heads,)),
         "halo_send": dma((3, heads)),
         "halo_recv": dma((3,)),
         "weight_send": dma((2, passes)),
         "weight_recv": dma((outer, CHUNKS)),
-        "log_send": dma((INNER,)),
-        "log_recv": dma((INNER,)),
-        "piece_send": dma((groups, INNER)),
-        "piece_recv": dma((groups, INNER)),
-        "chain_send": dma((groups,)),
+        "log_sems": dma((2,)),
+        "piece_send": dma((1,)),
+        "piece_recv": dma((groups,)),
+        "chain_send": dma((1,)),
         "chain_recv": dma((groups,)),
-        "start_send": dma((groups, INNER)),
-        "start_recv": dma((groups, INNER)),
-        "share_send": dma((groups, INNER)),
-        "share_recv": dma((groups, INNER)),
-        "term_send": dma((outer,)),
-        "term_recv": dma((heads, count)),
+        "start_send": dma((1,)),
+        "start_recv": dma((groups,)),
+        "share_send": dma((1,)),
+        "share_recv": dma((groups,)),
+        "near_recv": dma((2,)),
+        "term_send": dma((outer, column_halves(tile))),
+        "term_recv": dma((outer, column_halves(tile))),
     }
     names = list(inputs) + ["out"] + list(scratch)
     return pl.pallas_call(
         functools.partial(mixer_kernel, count, heads, names),
         out_shape=jax.ShapeDtypeStruct((rows, count * tile), dtype),
         in_specs=[spec for _, spec in inputs.values()],
-        out_specs=vmem,
+        out_specs=hbm,
         scratch_shapes=list(scratch.values()),
         compiler_params=pltpu.CompilerParams(
             collective_id=0, has_side_effects=True, vmem_limit_bytes=60 * 1024 * 1024

time: 168 us -> 162 us (0.964)
  Pallas kernels: 166 us -> 158 us
    pallas_call x1, Pallas kernels: 166 us -> 158 us  [per_device(): pl.pallas_call(functools.partial(mixer_kernel, count, heads, names), out_...]
where the time goes in v3:
time: 162 us; the launch traced here: 161 us
  Pallas kernels  158 us (98%)
  local copies, waits for them, and re-layouts  2.29 us (1%)
    pallas_call x1, Pallas kernels, per_device(): pl.pallas_call(functools.partial(mixer_kernel, count, heads, names), out_...  158 us

profile of v3, /device:TPU:17, one launch (start us, length us, event | category | flops | bytes accessed | tf_op | source)
XLA Modules:
  0.0 160.7 jit_solution(14228845261342891884)
XLA Ops:
  0.0 158.4 %mixer.1 = bf16[128,4096]{1,0:T(8,128)(2,1)} custom-call(bf16[128,8192]{1,0:T(8,128)(2,1)} %refs_0_.1, bf16[128,8192]{1,0:T(8,128)(2,1)} %refs_1_.1, bf16[128,1024]{1,0:T(8,128)(2,1)} %refs_2_.1, bf16[128,1024]{1,0:T(8,128)(2,1)} %refs_3_.1, bf16[128,128]{1,0:T(8,128)(2,1)} %refs_4_.1, bf16[4096,256]{1,0:T(8,128)(2,1)} %refs_5_.1, f32[1,64]{1,0:T(1,128)} %bitcast.6, ...), custom_call_target="tpu_custom_call" | custom-call | tf_op jit(solution)/shard_map/mixer/pallas_call | solution.py:913
  158.4 2.3 %copy.16 = bf16[128,4096]{1,0:T(8,128)(2,1)} copy(bf16[128,4096]{1,0:T(8,128)(2,1)} %mixer.1) | data formatting | bytes 2097152

commit v4 on v3

--- a/solution.py
+++ b/solution.py
@@ -11,7 +11,7 @@
 HEAD_DIM = 64
 STATE = 128
 SPAN = 128
-HALO = 16
+HALO = 8
 INNER = 4
 CHUNKS = 16
 STEPS = 8
@@ -32,7 +32,7 @@
         behind = level // 2 + 1
         if room >= 1:
             passes = max(passes, behind * min(room, 2))
-    return passes
+    return max(passes, outer - 1)
 
 
 def column_halves(tile):
@@ -42,9 +42,10 @@
 def column_orders(outer):
     edge = list(range(outer))
     if outer < 4:
-        return edge, edge
+        return edge, edge, edge
     first = [0, 2, outer - 1, 1]
-    return edge, first + [offset for offset in edge if offset not in first]
+    top = [0, 1] + list(range(outer - 1, 1, -1))
+    return edge, first + [offset for offset in edge if offset not in first], top
 
 
 def conv_silu(value, halo, taps_of, bias, padded, dtype):
@@ -221,14 +222,37 @@
         left = pl.multiple_of(lax.div(chunk, per_half) * half_cols, LANES)
         return r.wv.at[block, lines, pl.ds(left, half_cols)]
 
-    def weight_item(sign, which, chunk, kinds):
-        room = outer - 1 - level if sign > 0 else level
-        behind = lax.div(level if sign > 0 else outer - 1 - level, 2)
+    def down_item(which):
+        sign = -1
+        room = level
+        behind = lax.div(outer - 1 - level, 2)
         far = room >= 2
         hops = jnp.where(far, lax.div(which, 2), which)
         distance = jnp.where(far, 2 - lax.rem(which, 2), 1)
         exists = jnp.logical_and(room >= 1, hops <= behind)
-        edge = level == 0 if sign > 0 else level == outer - 1
+        edge = level == outer - 1
+        block = level - sign * 2 * hops
+        target = (level + sign * distance) * INNER + inner
+        fresh = jnp.logical_or(jnp.logical_not(far), distance == 2)
+        waits = jnp.logical_and(hops >= 1, fresh)
+        return exists, block, target, waits, far, edge
+
+    def up_item(which):
+        room = outer - 1 - level
+        own = which == 0
+        skips = jnp.logical_and(own, room >= 2)
+        bottom = jnp.where(skips, 2, 1)
+        first = jnp.logical_or(jnp.logical_and(own, room >= 2), which == 1)
+        some = jnp.logical_or(own, jnp.logical_and(level >= 2, which <= level))
+        exists = jnp.logical_and(room >= 1, jnp.where(level == 0, first, some))
+        block = jnp.where(level == 0, 0, jnp.where(own, level, which - 1))
+        target = (level + jnp.where(level == 0, bottom, 1)) * INNER + inner
+        waits = jnp.logical_and(level > 0, jnp.logical_not(own))
+        return exists, block, target, waits, room >= 2, level == 0
+
+    def weight_item(sign, which, chunk, kinds):
+        item = up_item(which) if sign > 0 else down_item(which)
+        exists, block, target, waits, far, edge = item
         if kinds is not None:
             way = "up" if sign > 0 else "down"
             chosen = jnp.bool_(False)
@@ -239,8 +263,6 @@
             if "mid " + way in kinds:
                 chosen = jnp.logical_or(chosen, jnp.logical_and(far, jnp.logical_not(edge)))
             exists = jnp.logical_and(exists, chosen)
-        block = level - sign * 2 * hops
-        target = (level + sign * distance) * INNER + inner
         view = chunk_view(block, chunk)
         copy = remote(
             view,
@@ -263,10 +285,8 @@
                 ).wait_send()
 
             return
-        fresh = jnp.logical_or(jnp.logical_not(far), distance == 2)
-        relayed = jnp.logical_and(jnp.logical_and(exists, hops >= 1), fresh)
-
-        @pl.when(relayed)
+
+        @pl.when(jnp.logical_and(exists, waits))
         def _():
             copy.wait_recv()
 
@@ -286,8 +306,9 @@
     def weight_arrived(block, chunk):
         below = block < level
         apart = jnp.where(below, level - block, block - level)
-        room = jnp.where(below, outer - 1 - level, level)
-        relayed = jnp.logical_and(lax.rem(apart, 2) == 0, room >= 1)
+        from_below = jnp.logical_and(level >= 2, level < outer - 1)
+        from_above = jnp.logical_and(lax.rem(apart, 2) == 0, level >= 1)
+        relayed = jnp.where(below, from_below, from_above)
 
         @pl.when(jnp.logical_and(apart > 0, jnp.logical_not(relayed)))
         def _():
@@ -305,7 +326,8 @@
             entry_copy(kind, 0, step).start()
     own_weight.wait()
     if passes > 1:
-        weight_pass(1, ("edge up", "edge down", "mid up"), 0, OPENING)
+        weight_pass(1, ("edge up", "edge down"), 0, OPENING)
+        weight_pass(0, ("mid up",), 0, OPENING)
     if passes:
         weight_pass(0, ("edge up", "edge down", "last up", "last down", "mid down"), 0, BEFORE)
         weight_pass(0, ("edge down", "last up", "last down", "mid down"), BEFORE)
@@ -539,7 +561,8 @@
 
     if passes > 1:
         with jax.named_scope("pass_one_early"):
-            weight_pass(1, ("edge up", "mid up"), OPENING, OPENING + FIRST)
+            weight_pass(1, ("edge up",), OPENING, OPENING + FIRST)
+            weight_pass(0, ("mid up",), OPENING)
             weight_pass(1, ("edge down",), OPENING)
             weight_pass(1, ("last down",), RELAYED)
             weight_pass(1, ("mid down",))
@@ -602,7 +625,6 @@
             @pl.when(g == min(LATE_GROUP, groups - 1))
             def _():
                 weight_pass(0, ("edge up",), BEFORE)
-                weight_pass(0, ("mid up",))
 
         return carry
 
@@ -611,24 +633,23 @@
 
     if passes > 1:
         with jax.named_scope("pass_one_late"):
-            weight_pass(1, ("edge up", "mid up"), OPENING + FIRST)
+            weight_pass(1, ("edge up",), OPENING + FIRST)
             weight_pass(1, ("last up",), BEFORE)
+            if outer > 4:
+                weight_pass(1, ("mid up",))
 
     def later_pass(which, carry):
         for part in ("edge", "last", "mid"):
             weight_pass(which, (part + " up", part + " down"))
         return carry
 
-    if passes > 2:
-        lax.fori_loop(2, passes, later_pass, 0)
-
-    edge_order, inner_order = column_orders(outer)
+    edge_order, inner_order, top_order = column_orders(outer)
     early_count = min(2, outer)
-    at_edge = jnp.logical_or(level == 0, level == outer - 1)
     direction = jnp.where(level < (outer + 1) // 2, 1, -1)
 
     def block_at(index):
-        offset = jnp.where(at_edge, edge_order[index], inner_order[index])
+        offset = jnp.where(level == outer - 1, top_order[index], inner_order[index])
+        offset = jnp.where(level == 0, edge_order[index], offset)
         return lax.rem(level + direction * offset + outer, outer)
 
     steps_per_group = width // step_rows
@@ -704,6 +725,10 @@
         share_copy(g, 2).wait_recv()
         forward_copy(g).start()
         return carry
+
+    if passes > 2:
+        with jax.named_scope("later"):
+            lax.fori_loop(2, passes, later_pass, 0)
 
     with jax.named_scope("pass_on"):
         lax.fori_loop(0, groups, pass_on, 0)

time: 162 us -> 158 us (0.975)
  the two profiles are of different devices: /device:TPU:17 before, /device:TPU:25 now
where the time goes in v4:
time: 158 us
  Pallas kernels  156 us (99%)
  local copies, waits for them, and re-layouts  2.29 us (1%)
    pallas_call x1, Pallas kernels, per_device(): pl.pallas_call(functools.partial(mixer_kernel, count, heads, names), out_...  156 us

profile of v4, /device:TPU:25, one launch (start us, length us, event | category | flops | bytes accessed | tf_op | source)
XLA Modules:
  0.0 157.9 jit_solution(2317503381614918408)
XLA Ops:
  0.0 155.6 %mixer.1 = bf16[128,4096]{1,0:T(8,128)(2,1)} custom-call(bf16[128,8192]{1,0:T(8,128)(2,1)} %refs_0_.1, bf16[128,8192]{1,0:T(8,128)(2,1)} %refs_1_.1, bf16[128,1024]{1,0:T(8,128)(2,1)} %refs_2_.1, bf16[128,1024]{1,0:T(8,128)(2,1)} %refs_3_.1, bf16[128,128]{1,0:T(8,128)(2,1)} %refs_4_.1, bf16[4096,256]{1,0:T(8,128)(2,1)} %refs_5_.1, f32[1,64]{1,0:T(1,128)} %bitcast.6, ...), custom_call_target="tpu_custom_call" | custom-call | tf_op jit(solution)/shard_map/mixer/pallas_call | solution.py:938
  155.7 2.3 %copy.16 = bf16[128,4096]{1,0:T(8,128)(2,1)} copy(bf16[128,4096]{1,0:T(8,128)(2,1)} %mixer.1) | data formatting | bytes 2097152
